TPU v7x, 32 devices: a whole 2x2x4 slice. The times are simulated.
32 devices in a mesh: rep: 4 (over x, y), dp: 8 (over z, core).
Axes of the slice: x: 2, y: 2, z: 4, core: 2. Of those that a mesh axis runs over, the one named last changes fastest.
Arguments:
- x: bfloat16 [32, 4096, 640], P(('rep', 'dp')), parts along dimension 0
- dy: bfloat16 [32, 4096, 640], P(('rep', 'dp')), parts along dimension 0
- w_gate: bfloat16 [2, 640, 3200], P(None, 'dp')
- w_up: bfloat16 [2, 640, 3200], P(None, 'dp')
- w_down: bfloat16 [2, 3200, 640], P(None, 'dp')
Outputs:
- output 1: bfloat16 [32, 4096, 640], P(('rep', 'dp')), parts along dimension 0
- output 2: bfloat16 [8, 640, 3200], P('rep', 'dp'), parts along dimension 0
- output 3: bfloat16 [8, 640, 3200], P('rep', 'dp'), parts along dimension 0
- output 4: bfloat16 [8, 3200, 640], P('rep', 'dp'), parts along dimension 0
There are 4 independent parts. A program takes and returns all parts, laid end to end along the dimension named above; an argument that names none is the same for every part.
All inputs are finite; a program needn't handle non-finite values.
Results may differ from a plain program's by a relative error of at most 0.018.
Values are sent between devices in bfloat16 or wider.
A program may use at most 2 GiB of HBM per device.

v0:
```python
import jax
import jax.numpy as jnp
from jax import lax

NAMES = ("w_gate", "w_up", "w_down")


def matmul(a, w):
    return jnp.dot(a, w, preferred_element_type=jnp.float32).astype(jnp.bfloat16)


def normed(h):
    wide = h.astype(jnp.float32)
    scale = lax.rsqrt(jnp.mean(wide**2, -1, keepdims=True) + 1e-6)
    return (wide * scale).astype(jnp.bfloat16)


def layer(h, w):
    a = normed(h)
    gate = jnp.dot(a, w["w_gate"], preferred_element_type=jnp.float32)
    up = jnp.dot(a, w["w_up"], preferred_element_type=jnp.float32)
    return h + matmul((jax.nn.silu(gate) * up).astype(jnp.bfloat16), w["w_down"])


def stack(weights, h):
    for number in range(weights["w_gate"].shape[0]):
        h = layer(h, {name: w[number] for name, w in weights.items()})
    return h


def solution(mesh):
    groups = mesh.shape["rep"]

    def step(x, dy, *weights):
        shape = x.shape
        x, dy = (t.reshape(groups, -1, *t.shape[1:]) for t in (x, dy))

        def of_a_group(x, dy):
            _, back = jax.vjp(stack, dict(zip(NAMES, weights, strict=True)), x)
            by_weights, by_x = back(dy)
            return (by_x, *(by_weights[name] for name in NAMES))

        by_x, *by_weights = jax.vmap(of_a_group)(x, dy)
        return (by_x.reshape(shape), *(t.reshape(-1, *t.shape[2:]) for t in by_weights))

    return step
```

profile of v0, /device:TPU:0, one launch (start us, length us, event | category | flops | bytes accessed | tf_op | source)
XLA Modules:
  0.0 1350.5 jit_solution(18111058076246359089)
XLA Ops:
  42.7 15.4 %all-gather.30.cloned.1.call-done = bf16[1,640,3200]{2,1,0:T(8,128)(2,1)} async-done(((bf16[1,80,3200]{2,1,0:T(8,128)(2,1)}), bf16[1,640,3200]{2,1,0:T(8,128)(2,1)}) %all-gather.30.cloned.1.call-update) | async-done | bytes 4096016 | tf_op jit(solution)/vmap(jvp())/squeeze | solution.py:27
  58.1 31.3 %fusion.239 = f32[4096,3200]{1,0:T(8,128)} fusion(bf16[1,640,3200]{2,1,0:T(8,128)(2,1)} %all-gather.30.cloned.1.call-done, bf16[1,4096,640]{2,1,0:T(8,128)(2,1)} %param.13, f32[4096]{0:T(1024)S(1)} %get-tuple-element.267), kind=kOutput, calls=%fused_computation.260 | convolution fusion | flops 16785080320 | bytes 61784064 | tf_op jit(solution)/vmap(jvp())/dot_general | solution.py:20
  89.4 15.2 %all-gather.32.cloned.1.call-done = bf16[1,640,3200]{2,1,0:T(8,128)(2,1)} async-done(((bf16[1,80,3200]{2,1,0:T(8,128)(2,1)}), bf16[1,640,3200]{2,1,0:T(8,128)(2,1)}) %all-gather.32.cloned.1.call-update) | async-done | bytes 4096016 | tf_op jit(solution)/vmap(jvp())/squeeze | solution.py:27
  104.6 51.0 %fusion.168 = (bf16[1,1,4096,3200]{3,2,1,0:T(8,128)(2,1)}, f32[4096,3200]{1,0:T(8,128)}) fusion(f32[4096,3200]{1,0:T(8,128)} %fusion.239, bf16[1,640,3200]{2,1,0:T(8,128)(2,1)} %all-gather.32.cloned.1.call-done, bf16[1,4096,640]{2,1,0:T(8,128)(2,1)} %param.13, f32[4096]{0:T(1024)S(1)} %get-tuple-element.267), kind=kOutput, calls=%fused_computation.195 | convolution fusion | flops 16863723520 | bytes 140427264 | tf_op jit(solution)/vmap(jvp())/dot_general | solution.py:21
  155.6 25.1 %fusion.182 = (f32[4096]{0:T(1024)S(1)}, bf16[1,1,4096,640]{2,3,1,0:T(8,128)(2,1)}) fusion(bf16[1,3200,640]{2,1,0:T(8,128)(2,1)} %all-gather.34.cloned.1.call-done, bf16[1,1,4096,3200]{3,2,1,0:T(8,128)(2,1)} %get-tuple-element.268, bf16[1,4096,640]{1,2,0:T(8,128)(2,1)} %copy.1), kind=kOutput, calls=%fused_computation.225 | convolution fusion | flops 16790319104 | bytes 40812544 | tf_op jit(solution)/vmap(jvp())/dot_general | solution.py:9
  180.7 33.3 %copy.4 = bf16[1,1,4096,3200]{2,3,1,0:T(8,128)(2,1)} copy(bf16[1,1,4096,3200]{3,2,1,0:T(8,128)(2,1)} %get-tuple-element.268) | data formatting | bytes 52428800
  221.5 28.0 %convolution_convert_fusion.1 = bf16[4096,3200]{1,0:T(8,128)(2,1)} fusion(bf16[1,4096,640]{2,1,0:T(8,128)(2,1)} %param.12, bf16[1,3200,640]{2,1,0:T(8,128)(2,1)} %all-gather.38.cloned.1.call-done), kind=kOutput, calls=%fused_computation.203 | convolution fusion | flops 16790323200 | bytes 35553280 | tf_op jit(solution)/vmap(transpose(jvp()))/dot_general | solution.py:9
  249.5 29.1 %fusion.224 = f32[4096,3200]{1,0:T(8,128)} fusion(bf16[1,1,4096,640]{2,3,1,0:T(8,128)(2,1)} %fusion.183, bf16[1,640,3200]{2,1,0:T(8,128)(2,1)} %all-gather.40.cloned.1.call-done), kind=kOutput, calls=%fused_computation.245 | convolution fusion | flops 16777216000 | bytes 61767680 | tf_op jit(solution)/vmap(jvp())/dot_general | solution.py:21
  278.6 11.3 all-gather.36.cloned.1.call-done
  289.9 83.4 %fusion.153 = (bf16[1,1,4096,3200]{3,2,1,0:T(8,128)(2,1)}, bf16[1,1,4096,3200]{3,2,1,0:T(8,128)(2,1)}, f32[4096,3200]{1,0:T(8,128)}) fusion(f32[4096,3200]{1,0:T(8,128)} %fusion.224, bf16[4096,3200]{1,0:T(8,128)(2,1)} %convolution_convert_fusion.1, bf16[1,640,3200]{2,1,0:T(8,128)(2,1)} %all-gather.36.cloned.1.call-done, bf16[1,1,4096,640]{2,3,1,0:T(8,128)(2,1)} %fusion.183), kind=kOutput, calls=%fused_computation.175 | convolution fusion | flops 16973824000 | bytes 192839680 | tf_op jit(solution)/vmap(jvp())/dot_general | solution.py:20
  373.4 42.2 %fusion.162 = bf16[1,1,4096,3200]{3,2,1,0:T(8,128)(2,1)} fusion(f32[4096,3200]{1,0:T(8,128)} %fusion.224, f32[4096,3200]{1,0:T(8,128)} %get-tuple-element.272), kind=kLoop, calls=%fused_computation.185 | loop fusion | flops 78643200 | bytes 131072000 | tf_op jit(solution)/vmap(jvp())/convert_element_type | solution.py:22
  415.6 32.8 %copy.2 = bf16[1,1,4096,3200]{2,3,1,0:T(8,128)(2,1)} copy(bf16[1,1,4096,3200]{3,2,1,0:T(8,128)(2,1)} %fusion.162) | data formatting | bytes 52428800
  448.4 107.7 %while.16 = (bf16[1,1,4096,3200]{2,3,1,0:T(8,128)(2,1)}, bf16[1,1,4096,640]{3,2,1,0:T(8,128)(2,1)}, f32[1,400,640]{2,1,0:T(8,128)S(1)}, f32[1,400,640]{2,1,0:T(8...) while((bf16[1,1,4096,3200]{2,3,1,0:T(8,128)(2,1)}, ...), condition=%wide.windowed_dot_general_cond_rs.4.clone, body=%wide.windowed_dot_general_body_rs.4.clone.sunk | while | flops 8416358400 | bytes 204636816 | solution.py:9
  463.6 11.4 collective-permute-done.16
  487.8 14.0 %collective-permute-done.18 = f32[1,400,640]{2,1,0:T(8,128)S(1)} collective-permute-done((f32[1,400,640]{2,1,0:T(8,128)S(1)}, f32[1,400,640]{2,1,0:T(8,128)S(1)}, u32[]{:S(2)}, u32[]{:S(2)}) %collective-permute-start.18) | collective-permute-done | bytes 1024032 | tf_op jit(solution)/vmap(transpose(jvp()))/dot_general | solution.py:9
  541.2 13.6 %collective-permute-done.18 = f32[1,400,640]{2,1,0:T(8,128)S(1)} collective-permute-done((f32[1,400,640]{2,1,0:T(8,128)S(1)}, f32[1,400,640]{2,1,0:T(8,128)S(1)}, u32[]{:S(2)}, u32[]{:S(2)}) %collective-permute-start.18) | collective-permute-done | bytes 1024032 | tf_op jit(solution)/vmap(transpose(jvp()))/dot_general | solution.py:9
  556.1 24.0 %fusion.188 = bf16[4096,640]{0,1:T(8,128)(2,1)} fusion(bf16[1,1,4096,3200]{3,2,1,0:T(8,128)(2,1)} %get-tuple-element.628, bf16[1,640,3200]{2,1,0:T(8,128)(2,1)} %all-gather.40.cloned.1.call-done), kind=kOutput, calls=%fused_computation.229 | convolution fusion | flops 16777216000 | bytes 35553280 | tf_op jit(solution)/vmap(transpose(jvp()))/dot_general | solution.py:21
  580.1 28.2 %fusion.184 = (f32[4096]{0:T(1024)S(1)}, bf16[1,1,4096,640]{2,3,1,0:T(8,128)(2,1)}) fusion(bf16[1,1,4096,640]{2,3,1,0:T(8,128)(2,1)} %get-tuple-element.271, bf16[4096,640]{0,1:T(8,128)(2,1)} %fusion.188, bf16[1,640,3200]{2,1,0:T(8,128)(2,1)} %all-gather.36.cloned.1.call-done, bf16[1,1,4096,3200]{3,2,1,0:T(8,128)(2,1)} %get-tuple-element.550), kind=kOutput, calls=%fused_computation.227 | convolution fusion | flops 16790319104 | bytes 46055424 | tf_op jit(solution)/vmap(transpose(jvp()))/dot_general | solution.py:20
  608.4 11.8 fusion.220
  628.1 109.3 %while.17 = (bf16[1,1,4096,3200]{2,3,1,0:T(8,128)(2,1)}, bf16[1,1,4096,640]{3,2,1,0:T(8,128)(2,1)}, f32[1,400,640]{2,1,0:T(8,128)S(1)}, f32[1,400,640]{2,1,0:T(8...) while((bf16[1,1,4096,3200]{2,3,1,0:T(8,128)(2,1)}, ...), condition=%wide.windowed_dot_general_cond_rs.5.clone, body=%wide.windowed_dot_general_body_rs.5.clone.sunk | while | flops 8416358400 | bytes 204636816 | solution.py:9
  666.2 15.4 %collective-permute-done.22 = f32[1,400,640]{2,1,0:T(8,128)S(1)} collective-permute-done((f32[1,400,640]{2,1,0:T(8,128)S(1)}, f32[1,400,640]{2,1,0:T(8,128)S(1)}, u32[]{:S(2)}, u32[]{:S(2)}) %collective-permute-start.22) | collective-permute-done | bytes 1024032 | tf_op jit(solution)/vmap(transpose(jvp()))/dot_general | solution.py:9
  723.1 13.1 collective-permute-done.22
  738.4 117.7 %while.14 = (bf16[1,1,4096,640]{2,3,1,0:T(8,128)(2,1)}, bf16[1,1,4096,3200]{3,2,1,0:T(8,128)(2,1)}, f32[1,80,3200]{2,1,0:T(8,128)S(1)}, f32[1,80,3200]{2,1,0:T(8...) while((bf16[1,1,4096,640]{2,3,1,0:T(8,128)(2,1)}, ...), condition=%wide.windowed_dot_general_cond_rs.2.clone, body=%wide.windowed_dot_general_body_rs.2.clone.sunk | while | flops 8395386880 | bytes 115507856 | solution.py:21
  745.8 11.6 fusion.321
  757.4 17.7 %collective-permute-done.8 = f32[1,80,3200]{2,1,0:T(8,128)} collective-permute-done((f32[1,80,3200]{2,1,0:T(8,128)S(1)}, f32[1,80,3200]{2,1,0:T(8,128)}, u32[]{:S(2)}, u32[]{:S(2)}) %collective-permute-start.8) | collective-permute-done | bytes 1024032 | tf_op jit(solution)/vmap(transpose(jvp()))/dot_general | solution.py:21
  780.3 11.1 fusion.323
  809.7 11.6 fusion.321
  833.7 11.1 fusion.323
  856.7 58.8 %fusion.155 = (bf16[1,1,4096,3200]{3,2,1,0:T(8,128)(2,1)}, bf16[1,1,4096,3200]{3,2,1,0:T(8,128)(2,1)}) fusion(f32[4096,3200]{1,0:T(8,128)} %fusion.239, f32[4096,3200]{1,0:T(8,128)} %get-tuple-element.269, bf16[1,3200,640]{2,1,0:T(8,128)(2,1)} %all-gather.34.cloned.1.call-done, bf16[1,1,4096,640]{2,3,1,0:T(8,128)(2,1)} %fusion.220), kind=kOutput, calls=%fused_computation.177 | convolution fusion | flops 16986931200 | bytes 166625280 | tf_op jit(solution)/vmap(transpose(jvp()))/dot_general | solution.py:9
  915.5 23.6 %fusion.194 = bf16[4096,640]{0,1:T(8,128)(2,1)} fusion(bf16[1,1,4096,3200]{3,2,1,0:T(8,128)(2,1)} %get-tuple-element.589, bf16[1,640,3200]{2,1,0:T(8,128)(2,1)} %all-gather.32.cloned.1.call-done), kind=kOutput, calls=%fused_computation.231 | convolution fusion | flops 16777216000 | bytes 35553280 | tf_op jit(solution)/vmap(transpose(jvp()))/dot_general | solution.py:21
  939.1 29.8 %fusion.181 = (bf16[1,1,4096,640]{2,3,1,0:T(8,128)(2,1)}, f32[4096]{0:T(1024)}, bf16[1,1,4096,640]{2,3,1,0:T(8,128)(2,1)}) fusion(bf16[1,4096,640]{1,2,0:T(8,128)(2,1)} %copy.1, f32[4096]{0:T(1024)S(1)} %bitcast.607, bf16[4096,640]{0,1:T(8,128)(2,1)} %fusion.194, bf16[1,640,3200]{2,1,0:T(8,128)(2,1)} %all-gather.30.cloned.1.call-done, ...), kind=kOutput, calls=%fused_computation.224 | convolution fusion | flops 16795561984 | bytes 51314688 | tf_op jit(solution)/vmap(transpose(jvp()))/dot_general | solution.py:20
  968.9 108.0 %while.15 = (bf16[1,1,4096,640]{2,3,1,0:T(8,128)(2,1)}, bf16[1,1,4096,3200]{3,2,1,0:T(8,128)(2,1)}, f32[1,80,3200]{2,1,0:T(8,128)S(1)}, f32[1,80,3200]{2,1,0:T(8...) while((bf16[1,1,4096,640]{2,3,1,0:T(8,128)(2,1)}, ...), condition=%wide.windowed_dot_general_cond_rs.3.clone, body=%wide.windowed_dot_general_body_rs.3.clone.sunk | while | flops 8395386880 | bytes 115507856 | solution.py:21
  976.4 11.6 fusion.329
  1001.7 11.1 fusion.331
  1012.8 10.9 collective-permute-done.14
  1031.3 11.6 fusion.329
  1055.4 11.1 fusion.331
  1078.9 110.2 %while.12 = (bf16[1,1,4096,640]{2,3,1,0:T(8,128)(2,1)}, bf16[1,1,4096,3200]{3,2,1,0:T(8,128)(2,1)}, f32[1,80,3200]{2,1,0:T(8,128)S(1)}, f32[1,80,3200]{2,1,0:T(8...) while((bf16[1,1,4096,640]{2,3,1,0:T(8,128)(2,1)}, ...), condition=%wide.windowed_dot_general_cond_rs.clone, body=%wide.windowed_dot_general_body_rs.clone.sunk | while | flops 8395386880 | bytes 115507856 | solution.py:20
  1087.2 11.6 fusion.305
  1111.0 11.1 fusion.307
  1143.0 11.6 fusion.305
  1166.7 11.1 fusion.307
  1189.1 105.6 %while.13 = (bf16[1,1,4096,640]{2,3,1,0:T(8,128)(2,1)}, bf16[1,1,4096,3200]{3,2,1,0:T(8,128)(2,1)}, f32[1,80,3200]{2,1,0:T(8,128)S(1)}, f32[1,80,3200]{2,1,0:T(8...) while((bf16[1,1,4096,640]{2,3,1,0:T(8,128)(2,1)}, ...), condition=%wide.windowed_dot_general_cond_rs.1.clone, body=%wide.windowed_dot_general_body_rs.1.clone.sunk | while | flops 8395386880 | bytes 115507856 | solution.py:20
  1196.7 11.6 fusion.313
  1220.4 11.1 fusion.315
  1249.4 11.6 fusion.313
  1273.1 11.1 fusion.315
  1295.6 11.8 fusion.219
  (329 shorter events, 447.2 us)
Async XLA Ops:
  7.2 51.0 %all-gather.30.cloned.1.call-start = ((), (), s32[]{:S(2)}) async-start(), calls=%async_computation | async-start | bytes 4608000 | tf_op jit(solution)/vmap(jvp())/squeeze | solution.py:27
  9.6 95.0 %all-gather.32.cloned.1.call-start = ((), (), s32[]{:S(2)}) async-start(), calls=%async_computation.1 | async-start | bytes 4608000 | tf_op jit(solution)/vmap(jvp())/squeeze | solution.py:27
  11.9 143.7 %all-gather.34.cloned.1.call-start = ((), (), s32[]{:S(2)}) async-start(), calls=%async_computation.2 | async-start | bytes 4608000 | tf_op jit(solution)/vmap(jvp())/squeeze | solution.py:27
  13.0 208.5 %all-gather.38.cloned.1.call-start = ((), (), s32[]{:S(2)}) async-start(), calls=%async_computation.4 | async-start | bytes 4608000 | tf_op jit(solution)/vmap(jvp())/squeeze | solution.py:27
  13.6 235.9 %all-gather.40.cloned.1.call-start = ((), (), s32[]{:S(2)}) async-start(), calls=%async_computation.5 | async-start | bytes 4608000 | tf_op jit(solution)/vmap(jvp())/squeeze | solution.py:27
  14.2 275.7 %all-gather.36.cloned.1.call-start = ((), (), s32[]{:S(2)}) async-start(), calls=%async_computation.3 | async-start | bytes 4608000 | tf_op jit(solution)/vmap(jvp())/squeeze | solution.py:27
  448.5 26.5 %collective-permute-start.16 = (f32[1,400,640]{2,1,0:T(8,128)S(1)}, f32[1,400,640]{2,1,0:T(8,128)}, u32[]{:S(2)}, u32[]{:S(2)}) collective-permute-start(f32[1,400,640]{2,1,0:T(8,128)S(1)} %broadcast_select_fusion.32), channel_id=39, source_target_pairs={{0,1},{1,2},{2,3},{3,4},{4,5},{5,6},{6,7},{7,0},{8,9},{9,10},{10,1... | collective-permute-start | bytes 3072008 | tf_op jit(solution)/vmap(transpose(jvp()))/dot_general | solution.py:9
  448.8 26.2 %collective-permute-start.17 = (f32[1,400,640]{2,1,0:T(8,128)S(1)}, f32[1,400,640]{2,1,0:T(8,128)S(1)}, u32[]{:S(2)}, u32[]{:S(2)}) collective-permute-start(f32[1,400,640]{2,1,0:T(8,128)S(1)} %broadcast_select_fusion.33), channel_id=38, source_target_pairs={{0,7},{1,0},{2,1},{3,2},{4,3},{5,4},{6,5},{7,6},{8,15},{9,8},{10,9... | collective-permute-start | bytes 3072008 | tf_op jit(solution)/vmap(transpose(jvp()))/dot_general | solution.py:9
  476.5 25.3 %collective-permute-start.18 = (f32[1,400,640]{2,1,0:T(8,128)S(1)}, f32[1,400,640]{2,1,0:T(8,128)S(1)}, u32[]{:S(2)}, u32[]{:S(2)}) collective-permute-start(f32[1,400,640]{2,1,0:T(8,128)S(1)} %get-tuple-element.497), channel_id=41, source_target_pairs={{0,1},{1,2},{2,3},{3,4},{4,5},{5,6},{6,7},{7,0},{8,9},{9,10},{10,1... | collective-permute-start | bytes 3072008 | tf_op jit(solution)/vmap(transpose(jvp()))/dot_general | solution.py:9
  476.5 25.2 %collective-permute-start.19 = (f32[1,400,640]{2,1,0:T(8,128)S(1)}, f32[1,400,640]{2,1,0:T(8,128)S(1)}, u32[]{:S(2)}, u32[]{:S(2)}) collective-permute-start(f32[1,400,640]{2,1,0:T(8,128)S(1)} %get-tuple-element.498), channel_id=40, source_target_pairs={{0,7},{1,0},{2,1},{3,2},{4,3},{5,4},{6,5},{7,6},{8,15},{9,8},{10,9... | collective-permute-start | bytes 3072008 | tf_op jit(solution)/vmap(transpose(jvp()))/dot_general | solution.py:9
  529.8 24.9 %collective-permute-start.18 = (f32[1,400,640]{2,1,0:T(8,128)S(1)}, f32[1,400,640]{2,1,0:T(8,128)S(1)}, u32[]{:S(2)}, u32[]{:S(2)}) collective-permute-start(f32[1,400,640]{2,1,0:T(8,128)S(1)} %get-tuple-element.497), channel_id=41, source_target_pairs={{0,1},{1,2},{2,3},{3,4},{4,5},{5,6},{6,7},{7,0},{8,9},{9,10},{10,1... | collective-permute-start | bytes 3072008 | tf_op jit(solution)/vmap(transpose(jvp()))/dot_general | solution.py:9
  529.9 24.9 %collective-permute-start.19 = (f32[1,400,640]{2,1,0:T(8,128)S(1)}, f32[1,400,640]{2,1,0:T(8,128)S(1)}, u32[]{:S(2)}, u32[]{:S(2)}) collective-permute-start(f32[1,400,640]{2,1,0:T(8,128)S(1)} %get-tuple-element.498), channel_id=40, source_target_pairs={{0,7},{1,0},{2,1},{3,2},{4,3},{5,4},{6,5},{7,6},{8,15},{9,8},{10,9... | collective-permute-start | bytes 3072008 | tf_op jit(solution)/vmap(transpose(jvp()))/dot_general | solution.py:9
  556.1 762.5 %collective-permute-start.28 = (f32[1,400,640]{2,1,0:T(8,128)}, f32[1,400,640]{2,1,0:T(8,128)}, u32[]{:S(2)}, u32[]{:S(2)}) collective-permute-start(f32[1,400,640]{2,1,0:T(8,128)} %get-tuple-element.45), channel_id=42, source_target_pairs={{0,1},{1,2},{2,3},{3,4},{4,5},{5,6},{6,7},{7,0},{8,9},{9,10},{10,1... | collective-permute-start | bytes 3072008 | tf_op jit(solution)/vmap(transpose(jvp()))/dot_general | solution.py:9
  628.4 25.0 %collective-permute-start.20 = (f32[1,400,640]{2,1,0:T(8,128)S(1)}, f32[1,400,640]{2,1,0:T(8,128)}, u32[]{:S(2)}, u32[]{:S(2)}) collective-permute-start(f32[1,400,640]{2,1,0:T(8,128)S(1)} %broadcast_select_fusion.34), channel_id=45, source_target_pairs={{0,1},{1,2},{2,3},{3,4},{4,5},{5,6},{6,7},{7,0},{8,9},{9,10},{10,1... | collective-permute-start | bytes 3072008 | tf_op jit(solution)/vmap(transpose(jvp()))/dot_general | solution.py:9
  654.9 26.7 %collective-permute-start.22 = (f32[1,400,640]{2,1,0:T(8,128)S(1)}, f32[1,400,640]{2,1,0:T(8,128)S(1)}, u32[]{:S(2)}, u32[]{:S(2)}) collective-permute-start(f32[1,400,640]{2,1,0:T(8,128)S(1)} %get-tuple-element.506), channel_id=47, source_target_pairs={{0,1},{1,2},{2,3},{3,4},{4,5},{5,6},{6,7},{7,0},{8,9},{9,10},{10,1... | collective-permute-start | bytes 3072008 | tf_op jit(solution)/vmap(transpose(jvp()))/dot_general | solution.py:9
  656.1 25.5 %collective-permute-start.23 = (f32[1,400,640]{2,1,0:T(8,128)S(1)}, f32[1,400,640]{2,1,0:T(8,128)S(1)}, u32[]{:S(2)}, u32[]{:S(2)}) collective-permute-start(f32[1,400,640]{2,1,0:T(8,128)S(1)} %get-tuple-element.507), channel_id=46, source_target_pairs={{0,7},{1,0},{2,1},{3,2},{4,3},{5,4},{6,5},{7,6},{8,15},{9,8},{10,9... | collective-permute-start | bytes 3072008 | tf_op jit(solution)/vmap(transpose(jvp()))/dot_general | solution.py:9
  684.1 26.2 %collective-permute-start.20 = (f32[1,400,640]{2,1,0:T(8,128)S(1)}, f32[1,400,640]{2,1,0:T(8,128)}, u32[]{:S(2)}, u32[]{:S(2)}) collective-permute-start(f32[1,400,640]{2,1,0:T(8,128)S(1)} %broadcast_select_fusion.34), channel_id=45, source_target_pairs={{0,1},{1,2},{2,3},{3,4},{4,5},{5,6},{6,7},{7,0},{8,9},{9,10},{10,1... | collective-permute-start | bytes 3072008 | tf_op jit(solution)/vmap(transpose(jvp()))/dot_general | solution.py:9
  685.3 25.0 %collective-permute-start.21 = (f32[1,400,640]{2,1,0:T(8,128)}, f32[1,400,640]{2,1,0:T(8,128)S(1)}, u32[]{:S(2)}, u32[]{:S(2)}) collective-permute-start(f32[1,400,640]{2,1,0:T(8,128)} %broadcast_select_fusion.35), channel_id=44, source_target_pairs={{0,7},{1,0},{2,1},{3,2},{4,3},{5,4},{6,5},{7,6},{8,15},{9,8},{10,9... | collective-permute-start | bytes 3072008 | tf_op jit(solution)/vmap(transpose(jvp()))/dot_general | solution.py:9
  737.4 582.5 %collective-permute-start.29 = (f32[1,400,640]{2,1,0:T(8,128)}, f32[1,400,640]{2,1,0:T(8,128)}, u32[]{:S(2)}, u32[]{:S(2)}) collective-permute-start(f32[1,400,640]{2,1,0:T(8,128)} %get-tuple-element.47), channel_id=48, source_target_pairs={{0,1},{1,2},{2,3},{3,4},{4,5},{5,6},{6,7},{7,0},{8,9},{9,10},{10,1... | collective-permute-start | bytes 3072008 | tf_op jit(solution)/vmap(transpose(jvp()))/dot_general | solution.py:9
  738.5 36.6 %collective-permute-start.8 = (f32[1,80,3200]{2,1,0:T(8,128)S(1)}, f32[1,80,3200]{2,1,0:T(8,128)}, u32[]{:S(2)}, u32[]{:S(2)}) collective-permute-start(f32[1,80,3200]{2,1,0:T(8,128)S(1)} %broadcast_select_fusion.28), channel_id=27, source_target_pairs={{0,1},{1,2},{2,3},{3,4},{4,5},{5,6},{6,7},{7,0},{8,9},{9,10},{10,1... | collective-permute-start | bytes 3072008 | tf_op jit(solution)/vmap(transpose(jvp()))/dot_general | solution.py:21
  739.7 35.5 %collective-permute-start.9 = (f32[1,80,3200]{2,1,0:T(8,128)}, f32[1,80,3200]{2,1,0:T(8,128)S(1)}, u32[]{:S(2)}, u32[]{:S(2)}) collective-permute-start(f32[1,80,3200]{2,1,0:T(8,128)} %broadcast_select_fusion.29), channel_id=26, source_target_pairs={{0,7},{1,0},{2,1},{3,2},{4,3},{5,4},{6,5},{7,6},{8,15},{9,8},{10,9... | collective-permute-start | bytes 3072008 | tf_op jit(solution)/vmap(transpose(jvp()))/dot_general | solution.py:21
  802.4 26.2 %collective-permute-start.8 = (f32[1,80,3200]{2,1,0:T(8,128)S(1)}, f32[1,80,3200]{2,1,0:T(8,128)}, u32[]{:S(2)}, u32[]{:S(2)}) collective-permute-start(f32[1,80,3200]{2,1,0:T(8,128)S(1)} %broadcast_select_fusion.28), channel_id=27, source_target_pairs={{0,1},{1,2},{2,3},{3,4},{4,5},{5,6},{6,7},{7,0},{8,9},{9,10},{10,1... | collective-permute-start | bytes 3072008 | tf_op jit(solution)/vmap(transpose(jvp()))/dot_general | solution.py:21
  803.7 24.9 %collective-permute-start.9 = (f32[1,80,3200]{2,1,0:T(8,128)}, f32[1,80,3200]{2,1,0:T(8,128)S(1)}, u32[]{:S(2)}, u32[]{:S(2)}) collective-permute-start(f32[1,80,3200]{2,1,0:T(8,128)} %broadcast_select_fusion.29), channel_id=26, source_target_pairs={{0,7},{1,0},{2,1},{3,2},{4,3},{5,4},{6,5},{7,6},{8,15},{9,8},{10,9... | collective-permute-start | bytes 3072008 | tf_op jit(solution)/vmap(transpose(jvp()))/dot_general | solution.py:21
  830.1 24.7 %collective-permute-start.10 = (f32[1,80,3200]{2,1,0:T(8,128)S(1)}, f32[1,80,3200]{2,1,0:T(8,128)S(1)}, u32[]{:S(2)}, u32[]{:S(2)}) collective-permute-start(f32[1,80,3200]{2,1,0:T(8,128)S(1)} %get-tuple-element.479), channel_id=29, source_target_pairs={{0,1},{1,2},{2,3},{3,4},{4,5},{5,6},{6,7},{7,0},{8,9},{9,10},{10,1... | collective-permute-start | bytes 3072008 | tf_op jit(solution)/vmap(transpose(jvp()))/dot_general | solution.py:21
  856.1 459.3 %collective-permute-start.26 = (f32[1,80,3200]{2,1,0:T(8,128)}, f32[1,80,3200]{2,1,0:T(8,128)}, u32[]{:S(2)}, u32[]{:S(2)}) collective-permute-start(f32[1,80,3200]{2,1,0:T(8,128)} %get-tuple-element.41), channel_id=30, source_target_pairs={{0,1},{1,2},{2,3},{3,4},{4,5},{5,6},{6,7},{7,0},{8,9},{9,10},{10,1... | collective-permute-start | bytes 3072008 | tf_op jit(solution)/vmap(transpose(jvp()))/dot_general | solution.py:21
  970.1 26.5 %collective-permute-start.12 = (f32[1,80,3200]{2,1,0:T(8,128)}, f32[1,80,3200]{2,1,0:T(8,128)}, u32[]{:S(2)}, u32[]{:S(2)}) collective-permute-start(f32[1,80,3200]{2,1,0:T(8,128)} %broadcast_select_fusion.30), channel_id=33, source_target_pairs={{0,1},{1,2},{2,3},{3,4},{4,5},{5,6},{6,7},{7,0},{8,9},{9,10},{10,1... | collective-permute-start | bytes 3072008 | tf_op jit(solution)/vmap(transpose(jvp()))/dot_general | solution.py:21
  970.2 26.4 %collective-permute-start.13 = (f32[1,80,3200]{2,1,0:T(8,128)S(1)}, f32[1,80,3200]{2,1,0:T(8,128)S(1)}, u32[]{:S(2)}, u32[]{:S(2)}) collective-permute-start(f32[1,80,3200]{2,1,0:T(8,128)S(1)} %broadcast_select_fusion.31), channel_id=32, source_target_pairs={{0,7},{1,0},{2,1},{3,2},{4,3},{5,4},{6,5},{7,6},{8,15},{9,8},{10,9... | collective-permute-start | bytes 3072008 | tf_op jit(solution)/vmap(transpose(jvp()))/dot_general | solution.py:21
  998.1 25.6 %collective-permute-start.14 = (f32[1,80,3200]{2,1,0:T(8,128)S(1)}, f32[1,80,3200]{2,1,0:T(8,128)S(1)}, u32[]{:S(2)}, u32[]{:S(2)}) collective-permute-start(f32[1,80,3200]{2,1,0:T(8,128)S(1)} %get-tuple-element.488), channel_id=35, source_target_pairs={{0,1},{1,2},{2,3},{3,4},{4,5},{5,6},{6,7},{7,0},{8,9},{9,10},{10,1... | collective-permute-start | bytes 3072008 | tf_op jit(solution)/vmap(transpose(jvp()))/dot_general | solution.py:21
  998.2 25.5 %collective-permute-start.15 = (f32[1,80,3200]{2,1,0:T(8,128)S(1)}, f32[1,80,3200]{2,1,0:T(8,128)S(1)}, u32[]{:S(2)}, u32[]{:S(2)}) collective-permute-start(f32[1,80,3200]{2,1,0:T(8,128)S(1)} %get-tuple-element.489), channel_id=34, source_target_pairs={{0,7},{1,0},{2,1},{3,2},{4,3},{5,4},{6,5},{7,6},{8,15},{9,8},{10,9... | collective-permute-start | bytes 3072008 | tf_op jit(solution)/vmap(transpose(jvp()))/dot_general | solution.py:21
  1025.1 25.2 %collective-permute-start.12 = (f32[1,80,3200]{2,1,0:T(8,128)}, f32[1,80,3200]{2,1,0:T(8,128)}, u32[]{:S(2)}, u32[]{:S(2)}) collective-permute-start(f32[1,80,3200]{2,1,0:T(8,128)} %broadcast_select_fusion.30), channel_id=33, source_target_pairs={{0,1},{1,2},{2,3},{3,4},{4,5},{5,6},{6,7},{7,0},{8,9},{9,10},{10,1... | collective-permute-start | bytes 3072008 | tf_op jit(solution)/vmap(transpose(jvp()))/dot_general | solution.py:21
  1025.1 25.1 %collective-permute-start.13 = (f32[1,80,3200]{2,1,0:T(8,128)S(1)}, f32[1,80,3200]{2,1,0:T(8,128)S(1)}, u32[]{:S(2)}, u32[]{:S(2)}) collective-permute-start(f32[1,80,3200]{2,1,0:T(8,128)S(1)} %broadcast_select_fusion.31), channel_id=32, source_target_pairs={{0,7},{1,0},{2,1},{3,2},{4,3},{5,4},{6,5},{7,6},{8,15},{9,8},{10,9... | collective-permute-start | bytes 3072008 | tf_op jit(solution)/vmap(transpose(jvp()))/dot_general | solution.py:21
  1051.8 24.9 %collective-permute-start.14 = (f32[1,80,3200]{2,1,0:T(8,128)S(1)}, f32[1,80,3200]{2,1,0:T(8,128)S(1)}, u32[]{:S(2)}, u32[]{:S(2)}) collective-permute-start(f32[1,80,3200]{2,1,0:T(8,128)S(1)} %get-tuple-element.488), channel_id=35, source_target_pairs={{0,1},{1,2},{2,3},{3,4},{4,5},{5,6},{6,7},{7,0},{8,9},{9,10},{10,1... | collective-permute-start | bytes 3072008 | tf_op jit(solution)/vmap(transpose(jvp()))/dot_general | solution.py:21
  1051.8 24.8 %collective-permute-start.15 = (f32[1,80,3200]{2,1,0:T(8,128)S(1)}, f32[1,80,3200]{2,1,0:T(8,128)S(1)}, u32[]{:S(2)}, u32[]{:S(2)}) collective-permute-start(f32[1,80,3200]{2,1,0:T(8,128)S(1)} %get-tuple-element.489), channel_id=34, source_target_pairs={{0,7},{1,0},{2,1},{3,2},{4,3},{5,4},{6,5},{7,6},{8,15},{9,8},{10,9... | collective-permute-start | bytes 3072008 | tf_op jit(solution)/vmap(transpose(jvp()))/dot_general | solution.py:21
  1079.9 26.0 %collective-permute-start = (f32[1,80,3200]{2,1,0:T(8,128)}, f32[1,80,3200]{2,1,0:T(8,128)}, u32[]{:S(2)}, u32[]{:S(2)}) collective-permute-start(f32[1,80,3200]{2,1,0:T(8,128)} %broadcast_select_fusion.24), channel_id=15, source_target_pairs={{0,1},{1,2},{2,3},{3,4},{4,5},{5,6},{6,7},{7,0},{8,9},{9,10},{10,1... | collective-permute-start | bytes 3072008 | tf_op jit(solution)/vmap(transpose(jvp()))/dot_general | solution.py:20
  1081.0 24.9 %collective-permute-start.1 = (f32[1,80,3200]{2,1,0:T(8,128)}, f32[1,80,3200]{2,1,0:T(8,128)S(1)}, u32[]{:S(2)}, u32[]{:S(2)}) collective-permute-start(f32[1,80,3200]{2,1,0:T(8,128)} %broadcast_select_fusion.25), channel_id=14, source_target_pairs={{0,7},{1,0},{2,1},{3,2},{4,3},{5,4},{6,5},{7,6},{8,15},{9,8},{10,9... | collective-permute-start | bytes 3072008 | tf_op jit(solution)/vmap(transpose(jvp()))/dot_general | solution.py:20
  1107.4 24.6 %collective-permute-start.2 = (f32[1,80,3200]{2,1,0:T(8,128)S(1)}, f32[1,80,3200]{2,1,0:T(8,128)S(1)}, u32[]{:S(2)}, u32[]{:S(2)}) collective-permute-start(f32[1,80,3200]{2,1,0:T(8,128)S(1)} %get-tuple-element.461), channel_id=17, source_target_pairs={{0,1},{1,2},{2,3},{3,4},{4,5},{5,6},{6,7},{7,0},{8,9},{9,10},{10,1... | collective-permute-start | bytes 3072008 | tf_op jit(solution)/vmap(transpose(jvp()))/dot_general | solution.py:20
  1135.7 26.0 %collective-permute-start = (f32[1,80,3200]{2,1,0:T(8,128)}, f32[1,80,3200]{2,1,0:T(8,128)}, u32[]{:S(2)}, u32[]{:S(2)}) collective-permute-start(f32[1,80,3200]{2,1,0:T(8,128)} %broadcast_select_fusion.24), channel_id=15, source_target_pairs={{0,1},{1,2},{2,3},{3,4},{4,5},{5,6},{6,7},{7,0},{8,9},{9,10},{10,1... | collective-permute-start | bytes 3072008 | tf_op jit(solution)/vmap(transpose(jvp()))/dot_general | solution.py:20
  1136.8 24.9 %collective-permute-start.1 = (f32[1,80,3200]{2,1,0:T(8,128)}, f32[1,80,3200]{2,1,0:T(8,128)S(1)}, u32[]{:S(2)}, u32[]{:S(2)}) collective-permute-start(f32[1,80,3200]{2,1,0:T(8,128)} %broadcast_select_fusion.25), channel_id=14, source_target_pairs={{0,7},{1,0},{2,1},{3,2},{4,3},{5,4},{6,5},{7,6},{8,15},{9,8},{10,9... | collective-permute-start | bytes 3072008 | tf_op jit(solution)/vmap(transpose(jvp()))/dot_general | solution.py:20
  1163.1 24.6 %collective-permute-start.2 = (f32[1,80,3200]{2,1,0:T(8,128)S(1)}, f32[1,80,3200]{2,1,0:T(8,128)S(1)}, u32[]{:S(2)}, u32[]{:S(2)}) collective-permute-start(f32[1,80,3200]{2,1,0:T(8,128)S(1)} %get-tuple-element.461), channel_id=17, source_target_pairs={{0,1},{1,2},{2,3},{3,4},{4,5},{5,6},{6,7},{7,0},{8,9},{9,10},{10,1... | collective-permute-start | bytes 3072008 | tf_op jit(solution)/vmap(transpose(jvp()))/dot_general | solution.py:20
  1190.3 25.0 %collective-permute-start.4 = (f32[1,80,3200]{2,1,0:T(8,128)}, f32[1,80,3200]{2,1,0:T(8,128)}, u32[]{:S(2)}, u32[]{:S(2)}) collective-permute-start(f32[1,80,3200]{2,1,0:T(8,128)} %broadcast_select_fusion.26), channel_id=21, source_target_pairs={{0,1},{1,2},{2,3},{3,4},{4,5},{5,6},{6,7},{7,0},{8,9},{9,10},{10,1... | collective-permute-start | bytes 3072008 | tf_op jit(solution)/vmap(transpose(jvp()))/dot_general | solution.py:20
  1190.4 24.9 %collective-permute-start.5 = (f32[1,80,3200]{2,1,0:T(8,128)S(1)}, f32[1,80,3200]{2,1,0:T(8,128)S(1)}, u32[]{:S(2)}, u32[]{:S(2)}) collective-permute-start(f32[1,80,3200]{2,1,0:T(8,128)S(1)} %broadcast_select_fusion.27), channel_id=20, source_target_pairs={{0,7},{1,0},{2,1},{3,2},{4,3},{5,4},{6,5},{7,6},{8,15},{9,8},{10,9... | collective-permute-start | bytes 3072008 | tf_op jit(solution)/vmap(transpose(jvp()))/dot_general | solution.py:20
  1216.8 24.9 %collective-permute-start.6 = (f32[1,80,3200]{2,1,0:T(8,128)S(1)}, f32[1,80,3200]{2,1,0:T(8,128)S(1)}, u32[]{:S(2)}, u32[]{:S(2)}) collective-permute-start(f32[1,80,3200]{2,1,0:T(8,128)S(1)} %get-tuple-element.470), channel_id=23, source_target_pairs={{0,1},{1,2},{2,3},{3,4},{4,5},{5,6},{6,7},{7,0},{8,9},{9,10},{10,1... | collective-permute-start | bytes 3072008 | tf_op jit(solution)/vmap(transpose(jvp()))/dot_general | solution.py:20
  1216.9 24.8 %collective-permute-start.7 = (f32[1,80,3200]{2,1,0:T(8,128)S(1)}, f32[1,80,3200]{2,1,0:T(8,128)S(1)}, u32[]{:S(2)}, u32[]{:S(2)}) collective-permute-start(f32[1,80,3200]{2,1,0:T(8,128)S(1)} %get-tuple-element.471), channel_id=22, source_target_pairs={{0,7},{1,0},{2,1},{3,2},{4,3},{5,4},{6,5},{7,6},{8,15},{9,8},{10,9... | collective-permute-start | bytes 3072008 | tf_op jit(solution)/vmap(transpose(jvp()))/dot_general | solution.py:20
  1243.0 25.0 %collective-permute-start.4 = (f32[1,80,3200]{2,1,0:T(8,128)}, f32[1,80,3200]{2,1,0:T(8,128)}, u32[]{:S(2)}, u32[]{:S(2)}) collective-permute-start(f32[1,80,3200]{2,1,0:T(8,128)} %broadcast_select_fusion.26), channel_id=21, source_target_pairs={{0,1},{1,2},{2,3},{3,4},{4,5},{5,6},{6,7},{7,0},{8,9},{9,10},{10,1... | collective-permute-start | bytes 3072008 | tf_op jit(solution)/vmap(transpose(jvp()))/dot_general | solution.py:20
  1243.1 24.9 %collective-permute-start.5 = (f32[1,80,3200]{2,1,0:T(8,128)S(1)}, f32[1,80,3200]{2,1,0:T(8,128)S(1)}, u32[]{:S(2)}, u32[]{:S(2)}) collective-permute-start(f32[1,80,3200]{2,1,0:T(8,128)S(1)} %broadcast_select_fusion.27), channel_id=20, source_target_pairs={{0,7},{1,0},{2,1},{3,2},{4,3},{5,4},{6,5},{7,6},{8,15},{9,8},{10,9... | collective-permute-start | bytes 3072008 | tf_op jit(solution)/vmap(transpose(jvp()))/dot_general | solution.py:20
  1269.5 24.9 %collective-permute-start.6 = (f32[1,80,3200]{2,1,0:T(8,128)S(1)}, f32[1,80,3200]{2,1,0:T(8,128)S(1)}, u32[]{:S(2)}, u32[]{:S(2)}) collective-permute-start(f32[1,80,3200]{2,1,0:T(8,128)S(1)} %get-tuple-element.470), channel_id=23, source_target_pairs={{0,1},{1,2},{2,3},{3,4},{4,5},{5,6},{6,7},{7,0},{8,9},{9,10},{10,1... | collective-permute-start | bytes 3072008 | tf_op jit(solution)/vmap(transpose(jvp()))/dot_general | solution.py:20
  1269.6 24.8 %collective-permute-start.7 = (f32[1,80,3200]{2,1,0:T(8,128)S(1)}, f32[1,80,3200]{2,1,0:T(8,128)S(1)}, u32[]{:S(2)}, u32[]{:S(2)}) collective-permute-start(f32[1,80,3200]{2,1,0:T(8,128)S(1)} %get-tuple-element.471), channel_id=22, source_target_pairs={{0,7},{1,0},{2,1},{3,2},{4,3},{5,4},{6,5},{7,6},{8,15},{9,8},{10,9... | collective-permute-start | bytes 3072008 | tf_op jit(solution)/vmap(transpose(jvp()))/dot_general | solution.py:20
  1315.4 26.7 %collective-permute-start.25 = (f32[1,80,3200]{2,1,0:T(8,128)}, f32[1,80,3200]{2,1,0:T(8,128)S(1)}, u32[]{:S(2)}, u32[]{:S(2)}) collective-permute-start(f32[1,80,3200]{2,1,0:T(8,128)} %copy-done.16), channel_id=24, source_target_pairs={{0,1},{1,2},{2,3},{3,4},{4,5},{5,6},{6,7},{7,0},{8,9},{9,10},{10,1... | collective-permute-start | bytes 3072008 | tf_op jit(solution)/vmap(transpose(jvp()))/dot_general | solution.py:20
  (62 other events, 1966.6 us)
Sparse Core Ops, SparseCore 0:
  9.7 48.4 all-gather.29
  59.8 44.7 all-gather.31
  106.2 44.7 all-gather.33
  152.5 44.7 all-gather.37
  198.8 44.7 all-gather.39
  245.1 44.7 all-gather.35
where the time goes:
time: 1360 us; the launch traced here: 1350 us
  matrix products  661 us (49%)
  waiting for transfers between devices  306 us (22%)
  other arithmetic  133 us (10%)
  local copies, waits for them, and re-layouts  124 us (9%)
  starting transfers between devices  87.2 us (6%)
  loops' own time  24.7 us (2%)
  between operations  14.8 us (1%)
    dot_general x12, matrix products, layer(): gate = jnp.dot(a, w['w_gate'], preferred_element_type=jnp.float32)  263 us
    dot_general x12, matrix products, layer(): up = jnp.dot(a, w['w_up'], preferred_element_type=jnp.float32)  218 us
    dot_general x11, matrix products, matmul(): jnp.dot(a, w, preferred_element_type=jnp.float32).astype(jnp.bfloat16)  179 us
    unnamed x67, local copies, waits for them, and re-layouts  110 us
    dot_general x18, waiting for transfers between devices, matmul(): jnp.dot(a, w, preferred_element_type=jnp.float32).astype(jnp.bfloat16)  94.8 us
    dot_general x18, waiting for transfers between devices, layer(): gate = jnp.dot(a, w['w_gate'], preferred_element_type=jnp.float32)  86.9 us
    dot_general x18, waiting for transfers between devices, layer(): up = jnp.dot(a, w['w_up'], preferred_element_type=jnp.float32)  80.7 us
    convert_element_type x1, other arithmetic, layer(): (jax.nn.silu(gate) * up).astype(jnp.bfloat16)  42.2 us
  transfers between devices with their start and end apart: 60, of which 29 were waited for; matrix products, arithmetic and copies ran while one was open for 55% of the time, Pallas kernels for 0%

commit v1 on v0

v1 whole, which is shorter than its diff:
```python
import functools

import jax
import jax.numpy as jnp
from jax import lax
from jax.experimental import pallas as pl
from jax.experimental.pallas import tpu as pltpu
from jax.sharding import PartitionSpec as P

TOKENS, D, FF = 4096, 640, 3200
BLOCK = 640
BLOCKS = FF // BLOCK
VMEM = 62 * 1024 * 1024
F32, BF16 = jnp.float32, jnp.bfloat16


def nn(a, b):
    return lax.dot_general(a, b, (((1,), (0,)), ((), ())), preferred_element_type=F32)


def nt(a, b):
    return lax.dot_general(a, b, (((1,), (1,)), ((), ())), preferred_element_type=F32)


def tn(a, b):
    return lax.dot_general(a, b, (((0,), (0,)), ((), ())), preferred_element_type=F32)


def params(*semantics):
    return pltpu.CompilerParams(dimension_semantics=semantics, vmem_limit_bytes=VMEM)


def cost(flops, nbytes):
    return pl.CostEstimate(flops=flops, bytes_accessed=nbytes, transcendentals=0)


MM = 2 * TOKENS * D * FF


def scale_of(wide):
    return lax.rsqrt(jnp.mean(wide * wide, -1, keepdims=True) + 1e-6)


ZS, CORES = 4, 2
GU_ROWS, D_ROWS = D // 8, FF // 8


def pieces_of():
    out = []
    for buffer in range(4):
        for n in range(10 if buffer % 2 == 0 else 5):
            width = 640 if buffer % 2 == 0 else 128
            out.append((buffer, pl.ds(n * width, width), n % 2))
    return out


PIECES = pieces_of()


def gate_up_kernel(sub, a_ref, gu0, d0, gu1, d1, gu_ref, p_ref, o0, o1, o2, o3, b0, b1, b2, b3, own_sem, out_sem, send_z, send_x, send_d, arrive, crossed):
    r, dp = lax.axis_index("rep"), lax.axis_index("dp")
    z, k = dp // 2, dp % 2
    relay = r % 2 == k
    side = r // 2
    buffers, outs, shards = (b0, b1, b2, b3), (o0, o1, o2, o3), (gu0, d0, gu1, d1)
    step = pl.program_id(0) * pl.num_programs(1) + pl.program_id(1)
    steps = BLOCKS * (TOKENS // a_ref.shape[0])
    count = len(PIECES)

    def send(q, at, to, sem, to_sem):
        ref = buffers[PIECES[q][0]].at[at, k, :, PIECES[q][1]]
        return pltpu.make_async_remote_copy(
            src_ref=ref, dst_ref=ref, send_sem=sem, recv_sem=to_sem, device_id=to, device_id_type=pl.DeviceIdType.MESH
        )

    def three(q, sem):
        ref = buffers[PIECES[q][0]].at[pl.ds(0, 3), 0, :, PIECES[q][1]]
        return pltpu.make_async_copy(ref, ref, sem)

    def relays(q):
        return jnp.logical_and(relay, side == PIECES[q][2])

    def along(q):
        @pl.when(relays(q))
        def _():
            for dz in (1, 2, 3):
                to = (r, lax.rem(z + dz, ZS) * 2 + k)
                send(q, z, to, send_z.at[q], arrive.at[q]).start()

    def across(q):
        @pl.when(relays(q))
        def _():
            three(q, arrive.at[q]).wait()
            for dr in (1, 2, 3):
                for dz in (1, 2, 3):
                    to = (lax.rem(r + dr, 4), dp)
                    send(q, lax.rem(z + dz, ZS), to, send_x.at[q, dr - 1], arrive.at[q]).start()

    def cross(q):
        ref = buffers[PIECES[q][0]].at[:, k, :, PIECES[q][1]]
        return pltpu.make_async_remote_copy(
            src_ref=ref,
            dst_ref=ref,
            send_sem=send_d.at[q],
            recv_sem=crossed.at[q],
            device_id=(r, z * 2 + 1 - k),
            device_id_type=pl.DeviceIdType.MESH,
        )

    def over(q):
        @pl.when(jnp.logical_not(relays(q)))
        def _():
            three(q, arrive.at[q]).wait()

        cross(q).start()

    def arrived(q):
        cross(q).wait_recv()

    def end(q):
        cross(q).wait_send()

        @pl.when(relays(q))
        def _():
            three(q, send_z.at[q]).wait()
            for dr in range(3):
                three(q, send_x.at[q, dr]).wait()

    def to_hbm(n):
        return pltpu.make_async_copy(buffers[n], outs[n], out_sem.at[n])

    @pl.when(step == 0)
    def _():
        own = [pltpu.make_async_copy(shards[n], buffers[n].at[z, k], own_sem.at[n]) for n in range(4)]
        for copy in own:
            copy.start()
        barrier = pltpu.get_barrier_semaphore()
        for n in (1, 2, 3):
            pl.semaphore_signal(
                barrier, inc=1, device_id=(r, lax.rem(z + n, ZS) * 2 + k), device_id_type=pl.DeviceIdType.MESH
            )
            pl.semaphore_signal(barrier, inc=1, device_id=(lax.rem(r + n, 4), dp), device_id_type=pl.DeviceIdType.MESH)
        pl.semaphore_signal(barrier, inc=1, device_id=(r, z * 2 + 1 - k), device_id_type=pl.DeviceIdType.MESH)
        pl.semaphore_wait(barrier, 7)
        for copy in own:
            copy.wait()
        for q in range(count):
            along(q)
        across(0)
        across(1)
        over(0)
        over(1)
        across(2)
        arrived(0)
        arrived(1)

    @pl.when(step == 1)
    def _():
        across(3)
        across(4)
        over(2)

    for s in range(2, steps):

        @pl.when(step == s)
        def _():
            across(s + 3)
            over(s + 1)
            arrived(s)

    cols = pl.ds(pl.multiple_of(pl.program_id(0) * (2 * BLOCK), 2 * BLOCK), 2 * BLOCK)
    w = b0[:, :, :, cols].reshape(D, 2 * BLOCK)
    for s in range(a_ref.shape[0] // sub):
        rows = pl.ds(s * sub, sub)
        gu = nn(a_ref[rows, :], w)
        gu_ref[rows, :] = gu
        gate, up = gu[:, :BLOCK], gu[:, BLOCK:]
        p_ref[rows, :] = (gate * jax.nn.sigmoid(gate) * up).astype(BF16)

    @pl.when(step == steps - 1)
    def _():
        for q in range(steps + 3, count):
            across(q)
            over(q - 2)
        over(count - 2)
        over(count - 1)
        for q in range(steps, count):
            arrived(q)
        for n in range(4):
            to_hbm(n).start()
        for q in range(count):
            end(q)
        for n in range(4):
            to_hbm(n).wait()


def gate_up(a, gu0, d0, gu1, d1, tile=1024, sub=1024):
    hbm = pl.BlockSpec(memory_space=pl.ANY)
    wide = (ZS, CORES, GU_ROWS, 2 * FF)
    tall = (ZS, CORES, D_ROWS, D)
    count = len(PIECES)
    dma = pltpu.SemaphoreType.DMA
    return pl.pallas_call(
        functools.partial(gate_up_kernel, sub),
        grid=(BLOCKS, TOKENS // tile),
        in_specs=[pl.BlockSpec((tile, D), lambda j, i: (i, 0)), hbm, hbm, hbm, hbm],
        out_specs=[
            pl.BlockSpec((tile, 2 * BLOCK), lambda j, i: (i, j)),
            pl.BlockSpec((tile, BLOCK), lambda j, i: (i, j)),
            hbm,
            hbm,
            hbm,
            hbm,
        ],
        out_shape=[
            jax.ShapeDtypeStruct((TOKENS, 2 * FF), F32),
            jax.ShapeDtypeStruct((TOKENS, FF), BF16),
            jax.ShapeDtypeStruct(wide, BF16),
            jax.ShapeDtypeStruct(tall, BF16),
            jax.ShapeDtypeStruct(wide, BF16),
            jax.ShapeDtypeStruct(tall, BF16),
        ],
        scratch_shapes=[
            pltpu.VMEM(wide, BF16),
            pltpu.VMEM(tall, BF16),
            pltpu.VMEM(wide, BF16),
            pltpu.VMEM(tall, BF16),
            dma((4,)),
            dma((4,)),
            dma((count,)),
            dma((count, 3)),
            dma((count,)),
            dma((count,)),
            dma((count,)),
        ],
        compiler_params=pltpu.CompilerParams(
            dimension_semantics=("arbitrary", "arbitrary"), vmem_limit_bytes=VMEM, collective_id=0, has_side_effects=True
        ),
        cost_estimate=cost(2 * MM, TOKENS * FF * 10),
        name="gate_up",
    )(a, gu0, d0, gu1, d1)


def down_kernel(p_ref, w_ref, h_ref, out_ref, a_ref):
    y = nn(p_ref[...], w_ref[...]).astype(BF16)
    h = h_ref[...] + y
    out_ref[...] = h
    wide = h.astype(F32)
    a_ref[...] = (wide * scale_of(wide)).astype(BF16)


def down(p, w, h, tile=512):
    row = pl.BlockSpec((tile, D), lambda i: (i, 0))
    return pl.pallas_call(
        down_kernel,
        grid=(TOKENS // tile,),
        in_specs=[
            pl.BlockSpec((tile, FF), lambda i: (i, 0)),
            pl.BlockSpec((FF, D), lambda i: (0, 0), pipeline_mode=pl.Buffered(1)),
            row,
        ],
        out_specs=[row, row],
        out_shape=[jax.ShapeDtypeStruct((TOKENS, D), BF16)] * 2,
        compiler_params=params("arbitrary"),
        cost_estimate=cost(MM, TOKENS * FF * 2),
        name="down",
    )(p, w, h)


def back_kernel(sub, again, dy_ref, wd_ref, a_ref, gu_ref, dgu_ref, dw_ref, dd_ref, acc, accd, p_ref):
    i = pl.program_id(1)

    @pl.when(i == 0)
    def _():
        acc[...] = jnp.zeros_like(acc)
        accd[...] = jnp.zeros_like(accd)

    for s in range(dy_ref.shape[0] // sub):
        rows = pl.ds(s * sub, sub)
        dp = nt(dy_ref[rows, :], wd_ref[...]).astype(BF16).astype(F32)
        if again:
            gu = nn(a_ref[rows, :], gu_ref[...])
            gate, up = gu[:, :BLOCK], gu[:, BLOCK:]
        else:
            gate, up = gu_ref[rows, :BLOCK], gu_ref[rows, BLOCK:]
        sig = jax.nn.sigmoid(gate)
        silu = gate * sig
        p_ref[rows, :] = (silu * up).astype(BF16)
        dgu_ref[rows, :BLOCK] = (dp * up * (sig * (1.0 + gate * (1.0 - sig)))).astype(BF16)
        dgu_ref[rows, BLOCK:] = (dp * silu).astype(BF16)
    acc[...] += tn(a_ref[...], dgu_ref[...])
    accd[...] += tn(p_ref[...], dy_ref[...])

    @pl.when(i == pl.num_programs(1) - 1)
    def _():
        dw_ref[...] = acc[...].astype(BF16)
        dd_ref[...] = accd[...].astype(BF16)


def back(dy, wd, a, gu, again, first, blocks, tile=1024, sub=512):
    return pl.pallas_call(
        functools.partial(back_kernel, sub, again),
        grid=(blocks, TOKENS // tile),
        in_specs=[
            pl.BlockSpec((tile, D), lambda j, i: (i, 0)),
            pl.BlockSpec((BLOCK, D), lambda j, i: (first + j, 0)),
            pl.BlockSpec((tile, D), lambda j, i: (i, 0)),
            pl.BlockSpec((D, 2 * BLOCK), lambda j, i: (0, first + j))
            if again
            else pl.BlockSpec((tile, 2 * BLOCK), lambda j, i: (i, first + j)),
        ],
        out_specs=[
            pl.BlockSpec((tile, 2 * BLOCK), lambda j, i: (i, j)),
            pl.BlockSpec((D, 2 * BLOCK), lambda j, i: (0, j)),
            pl.BlockSpec((BLOCK, D), lambda j, i: (j, 0)),
        ],
        out_shape=[
            jax.ShapeDtypeStruct((TOKENS, 2 * BLOCK * blocks), BF16),
            jax.ShapeDtypeStruct((D, 2 * BLOCK * blocks), BF16),
            jax.ShapeDtypeStruct((BLOCK * blocks, D), BF16),
        ],
        scratch_shapes=[
            pltpu.VMEM((D, 2 * BLOCK), F32),
            pltpu.VMEM((BLOCK, D), F32),
            pltpu.VMEM((tile, BLOCK), BF16),
        ],
        compiler_params=params("arbitrary", "arbitrary"),
        cost_estimate=cost((6 if again else 4) * MM * blocks // BLOCKS, TOKENS * FF * (4 if again else 12) * blocks // BLOCKS),
        name="back",
    )(dy, wd, a, gu)


def grad_in_kernel(split, one_ref, two_ref, w_ref, h_ref, dy_ref, dh_ref):
    da = nt(one_ref[...], w_ref[:, :split]) + nt(two_ref[...], w_ref[:, split:])
    da = da.astype(BF16).astype(F32)
    wide = h_ref[...].astype(F32)
    scale = scale_of(wide)
    dot = jnp.mean(da * wide, -1, keepdims=True)
    by_wide = da * scale - wide * (scale * scale * scale * dot)
    dh_ref[...] = dy_ref[...] + by_wide.astype(BF16)


def grad_in(one, two, w, h, dy, tile=512):
    row = pl.BlockSpec((tile, D), lambda i: (i, 0))
    split = one.shape[1]
    return pl.pallas_call(
        functools.partial(grad_in_kernel, split),
        grid=(TOKENS // tile,),
        in_specs=[
            pl.BlockSpec((tile, split), lambda i: (i, 0)),
            pl.BlockSpec((tile, 2 * FF - split), lambda i: (i, 0)),
            pl.BlockSpec((D, 2 * FF), lambda i: (0, 0), pipeline_mode=pl.Buffered(1)),
            row,
            row,
        ],
        out_specs=row,
        out_shape=jax.ShapeDtypeStruct((TOKENS, D), BF16),
        compiler_params=params("arbitrary"),
        cost_estimate=cost(2 * MM, TOKENS * FF * 4),
        name="grad_in",
    )(one, two, w, h, dy)


def normed(h):
    wide = h.astype(F32)
    return (wide * scale_of(wide)).astype(BF16)


def beside(gate, up):
    parts = []
    for j in range(BLOCKS):
        cols = slice(j * BLOCK, (j + 1) * BLOCK)
        parts += [gate[:, cols], up[:, cols]]
    return jnp.concatenate(parts, 1)


def apart(both):
    parts = [both[:, j * BLOCK : (j + 1) * BLOCK] for j in range(2 * BLOCKS)]
    return jnp.concatenate(parts[0::2], 1), jnp.concatenate(parts[1::2], 1)


def scatter(dw):
    return lax.psum_scatter(dw, "dp", scatter_dimension=0, tiled=True)


SPLIT = 2


def solution(mesh):
    def backward(dy, wd, a, gu, again, w, h):
        one, dw_one, dd_one = back(dy, wd, a, gu, again, 0, SPLIT)
        dy, dw_one, dd_one = lax.optimization_barrier((dy, dw_one, dd_one))
        two, dw_two, dd_two = back(dy, wd, a, gu, again, SPLIT, BLOCKS - SPLIT)
        dy, dw_two, dd_two = lax.optimization_barrier((dy, dw_two, dd_two))
        by_gu = jnp.concatenate([scatter(dw_one), scatter(dw_two)], 1)
        by_d = scatter(jnp.concatenate([dd_one, dd_two], 0))
        return grad_in(one, two, w, h, dy), apart(by_gu), by_d

    def step(x, dy, w_gate, w_up, w_down):
        h0, dy = x[0], dy[0]
        a0 = normed(h0)
        gu0, p0, w0, d0, w1, d1 = gate_up(a0, beside(w_gate[0], w_up[0]), w_down[0], beside(w_gate[1], w_up[1]), w_down[1])
        w0, w1 = w0.reshape(D, 2 * FF), w1.reshape(D, 2 * FF)
        d0, d1 = d0.reshape(FF, D), d1.reshape(FF, D)
        h1, a1 = down(p0, d0, h0)
        dh1, (g1, u1), by_d1 = backward(dy, d1, a1, w1, True, w1, h1)
        dx, (g0, u0), by_d0 = backward(dh1, d0, a0, gu0, False, w0, h0)
        return dx[None], jnp.stack([g0, g1]), jnp.stack([u0, u1]), jnp.stack([by_d0, by_d1])

    tokens = P(("rep", "dp"), None, None)
    weights = P(None, "dp", None)
    return jax.shard_map(
        step,
        mesh=mesh,
        in_specs=(tokens, tokens, weights, weights, weights),
        out_specs=(tokens,) + (P("rep", "dp", None),) * 3,
        check_vma=False,
    )
```

time: 1360 us -> 710 us (0.52)
  matrix products: 661 us -> 0 us
  Pallas kernels: 0 us -> 525 us
  waiting for transfers between devices: 306 us -> 130 us
  other arithmetic: 133 us -> 19.4 us
  local copies, waits for them, and re-layouts: 124 us -> 12 us
  starting transfers between devices: 87.2 us -> 0.24 us
  loops' own time: 24.7 us -> 0 us
    dot_general x35 -> x0, matrix products: 661 us -> none  [the longest x12 263 us: layer(): gate = jnp.dot(a, w['w_gate'], preferred_element_type=jnp.float32)]
    pallas_call x0 -> x8, Pallas kernels: none -> 525 us  [the longest x4 251 us: back(): pl.pallas_call(functools.partial(back_kernel, sub, again), grid=(blocks,...]
    dot_general x54 -> x0, waiting for transfers between devices: 262 us -> none  [the longest x18 94.8 us: matmul(): jnp.dot(a, w, preferred_element_type=jnp.float32).astype(jnp.bfloat16)]
    reduce_scatter x0 -> x6, waiting for transfers between devices: none -> 129 us  [scatter(): return lax.psum_scatter(dw, 'dp', scatter_dimension=0, tiled=True)]
    unnamed x67 -> x43, local copies, waits for them, and re-layouts: 110 us -> 8.65 us
    dot_general x54 -> x0, starting transfers between devices: 87 us -> none  [the longest x18 29.4 us: layer(): up = jnp.dot(a, w['w_up'], preferred_element_type=jnp.float32)]
    dot_general x56 -> x0, other arithmetic: 47.7 us -> none
    convert_element_type x2 -> x1, other arithmetic: 48.4 us -> 3.3 us  [normed(): return (wide * scale_of(wide)).astype(BF16)]
  transfers between devices with their start and end apart: 60 -> 6, of which waited for: 29 -> 3; matrix products, arithmetic and copies ran while one was open for 55% -> 2% of each run, Pallas kernels for 0% -> 42%
where the time goes in v1:
time: 710 us; the launch traced here: 701 us
  Pallas kernels  525 us (74%)
  waiting for transfers between devices  130 us (18%)
  other arithmetic  19.4 us (3%)
  between operations  14.9 us (2%)
  local copies, waits for them, and re-layouts  12 us (2%)
    pallas_call x4, Pallas kernels, back(): pl.pallas_call(functools.partial(back_kernel, sub, again), grid=(blocks,...  251 us
    pallas_call x1, Pallas kernels, gate_up(): pl.pallas_call(functools.partial(gate_up_kernel, sub), grid=(BLOCKS, TOKE...  140 us
    reduce_scatter x6, waiting for transfers between devices, scatter(): return lax.psum_scatter(dw, 'dp', scatter_dimension=0, tiled=True)  129 us
    pallas_call x2, Pallas kernels, grad_in(): pl.pallas_call(functools.partial(grad_in_kernel, split), grid=(TOKENS //...  105 us
    pallas_call x1, Pallas kernels, down(): pl.pallas_call(down_kernel, grid=(TOKENS // tile,), in_specs=[pl.BlockSpe...  28.7 us
  transfers between devices with their start and end apart: 6, of which 3 were waited for; matrix products, arithmetic and copies ran while one was open for 2% of the time, Pallas kernels for 42%

profile of v1, /device:TPU:0, one launch (start us, length us, event | category | flops | bytes accessed | tf_op | source)
XLA Modules:
  0.0 701.5 jit_solution(8286412642810243680)
XLA Ops:
  7.2 0.0 reduce-scatter.11.cloned.1.call-start
  7.2 0.0 slice-start
  7.2 3.7 fusion
  11.0 0.1 slice_bitcast_fusion.2
  11.1 0.0 slice-start.1
  11.2 0.1 slice_bitcast_fusion.1
  11.7 0.5 copy-done.4
  12.2 1.2 slice_bitcast_fusion
  13.4 3.3 fusion.1.a_ref
  16.7 140.3 %gate_up.1 = (f32[4096,6400]{1,0:T(8,128)}, bf16[4096,3200]{1,0:T(8,128)(2,1)}, bf16[4,2,80,6400]{3,2,1,0:T(8,128)(2,1)}, bf16[4,2,400,640]{3,2,1,0:T(8,128)(2,1...) custom-call(bf16[4096,640]{1,0:T(8,128)(2,1)} %fusion.1.a_ref, bf16[80,6400]{1,0:T(8,128)(2,1)} %copy-done.5, ...), custom_call_target="tpu_custom_call" | custom-call | flops 33554432000 | bytes 131072000 | tf_op jit(solution)/shard_map/gate_up/pallas_call | solution.py:203
  157.0 28.7 %down.1 = (bf16[4096,640]{1,0:T(8,128)(2,1)}, bf16[4096,640]{1,0:T(8,128)(2,1)}) custom-call(bf16[4096,3200]{1,0:T(8,128)(2,1)} %get-tuple-element.37.p_ref, bf16[3200,640]{1,0:T(8,128)(2,1)} %bitcast.31, bf16[4096,640]{1,0:T(8,128)(2,1)} %bitcast.27), custom_call_target="tpu_custom_call" | custom-call | flops 16777216000 | bytes 26214400 | tf_op jit(solution)/shard_map/down/pallas_call | solution.py:254
  185.7 58.5 %back.4 = (bf16[4096,2560]{1,0:T(8,128)(2,1)}, bf16[640,2560]{1,0:T(8,128)(2,1)}, bf16[1280,640]{1,0:T(8,128)(2,1)}) custom-call(bf16[4096,640]{1,0:T(8,128)(2,1)} %bitcast.40, bf16[3200,640]{1,0:T(8,128)(2,1)} %bitcast.48, bf16[4096,640]{1,0:T(8,128)(2,1)} %get-tuple-element.39.a_ref, bf16[640,6400]{1,0:T(8,128)(2,1)} %bitcast.44), custom_call_target="tpu_custom_call" | custom-call | flops 40265318400 | bytes 20971520 | tf_op jit(solution)/shard_map/back/pallas_call | solution.py:301
  244.2 0.0 reduce-scatter.11.cloned.1.call-update
  244.2 0.0 reduce-scatter.7.cloned.1.call-start
  244.2 85.4 %back.5 = (bf16[4096,3840]{1,0:T(8,128)(2,1)}, bf16[640,3840]{1,0:T(8,128)(2,1)}, bf16[1920,640]{1,0:T(8,128)(2,1)}) custom-call(bf16[4096,640]{1,0:T(8,128)(2,1)} %bitcast.41, bf16[3200,640]{1,0:T(8,128)(2,1)} %bitcast.49, bf16[4096,640]{1,0:T(8,128)(2,1)} %get-tuple-element.39.a_ref, bf16[640,6400]{1,0:T(8,128)(2,1)} %bitcast.45), custom_call_target="tpu_custom_call" | custom-call | flops 60397977600 | bytes 31457280 | tf_op jit(solution)/shard_map/back/pallas_call | solution.py:301
  329.7 52.5 %grad_in.2.dy_ref = bf16[4096,640]{1,0:T(8,128)(2,1)} custom-call(bf16[4096,2560]{1,0:T(8,128)(2,1)} %get-tuple-element.41.one_ref, bf16[4096,3840]{1,0:T(8,128)(2,1)} %get-tuple-element.45.two_ref, bf16[640,6400]{1,0:T(8,128)(2,1)} %bitcast.46, bf16[4096,640]{1,0:T(8,128)(2,1)} %get-tuple-element.46.h_ref, bf16[4096,640]{1,0:T(8,128)(2,1)} %bitcast.42), custom_call_target="tpu_custom_call" | custom-call | flops 33554432000 | bytes 52428800 | tf_op jit(solution)/shard_map/grad_in/pallas_call | solution.py:346
  382.2 44.0 %back.6 = (bf16[4096,2560]{1,0:T(8,128)(2,1)}, bf16[640,2560]{1,0:T(8,128)(2,1)}, bf16[1280,640]{1,0:T(8,128)(2,1)}) custom-call(bf16[4096,640]{1,0:T(8,128)(2,1)} %grad_in.2.dy_ref, bf16[3200,640]{1,0:T(8,128)(2,1)} %bitcast.32, bf16[4096,640]{1,0:T(8,128)(2,1)} %fusion.1.a_ref, f32[4096,6400]{1,0:T(8,128)} %get-tuple-element.50.gu_ref), custom_call_target="tpu_custom_call" | custom-call | flops 26843545600 | bytes 62914560 | tf_op jit(solution)/shard_map/back/pallas_call | solution.py:301
  426.2 0.0 reduce-scatter.7.cloned.1.call-update
  426.2 0.0 reduce-scatter.17.cloned.1.call-start
  426.2 4.0 pad_maximum_fusion.1
  430.2 0.0 reduce-scatter.17.cloned.1.call-update
  430.3 0.0 reduce-scatter.15.cloned.1.call-start
  430.3 62.8 %back.7 = (bf16[4096,3840]{1,0:T(8,128)(2,1)}, bf16[640,3840]{1,0:T(8,128)(2,1)}, bf16[1920,640]{1,0:T(8,128)(2,1)}) custom-call(bf16[4096,640]{1,0:T(8,128)(2,1)} %grad_in.2.dy_ref, bf16[3200,640]{1,0:T(8,128)(2,1)} %bitcast.33, bf16[4096,640]{1,0:T(8,128)(2,1)} %fusion.1.a_ref, f32[4096,6400]{1,0:T(8,128)} %get-tuple-element.50.gu_ref), custom_call_target="tpu_custom_call" | custom-call | flops 40265318400 | bytes 94371840 | tf_op jit(solution)/shard_map/back/pallas_call | solution.py:301
  493.1 4.0 pad_maximum_fusion
  497.1 0.0 reduce-scatter.15.cloned.1.call-update
  497.1 0.0 reduce-scatter.13.cloned.1.call-start
  497.1 0.5 reduce-scatter.13.cloned.1.call-update
  497.7 0.0 reduce-scatter.9.cloned.1.call-start
  497.7 0.5 reduce-scatter.9.cloned.1.call-update
  498.2 52.6 %grad_in.3 = bf16[4096,640]{1,0:T(8,128)(2,1)} custom-call(bf16[4096,2560]{1,0:T(8,128)(2,1)} %get-tuple-element.51.one_ref, bf16[4096,3840]{1,0:T(8,128)(2,1)} %get-tuple-element.55.two_ref, bf16[640,6400]{1,0:T(8,128)(2,1)} %bitcast.43, bf16[4096,640]{1,0:T(8,128)(2,1)} %bitcast.28, bf16[4096,640]{1,0:T(8,128)(2,1)} %grad_in.2.dy_ref), custom_call_target="tpu_custom_call" | custom-call | flops 33554432000 | bytes 52428800 | tf_op jit(solution)/shard_map/grad_in/pallas_call | solution.py:346
  550.8 1.0 slice_dynamic-update-slice_fusion.4
  551.8 0.0 reduce-scatter.7.cloned.1.call-done
  551.8 1.0 slice_dynamic-update-slice_fusion.9
  552.8 1.0 slice_dynamic-update-slice_fusion.3
  553.8 1.0 slice_dynamic-update-slice_fusion.8
  554.8 0.0 reduce-scatter.17.cloned.1.call-done
  554.8 19.0 %reduce-scatter.15.cloned.1.call-done = bf16[400,640]{1,0:T(8,128)(2,1)} async-done(((bf16[3200,640]{1,0:T(8,128)(2,1)}), bf16[400,640]{1,0:T(8,128)(2,1)}) %reduce-scatter.15.cloned.1.call-update) | async-done | bytes 512016 | tf_op jit(solution)/shard_map/reduce_scatter | solution.py:383
  573.8 2.3 pad_maximum_fusion.4
  576.0 55.4 %reduce-scatter.13.cloned.1.call-done = bf16[80,3840]{1,0:T(8,128)(2,1)} async-done(((bf16[640,3840]{1,0:T(8,128)(2,1)}), bf16[80,3840]{1,0:T(8,128)(2,1)}) %reduce-scatter.13.cloned.1.call-update) | async-done | bytes 614416 | tf_op jit(solution)/shard_map/reduce_scatter | solution.py:383
  631.4 1.0 slice_dynamic-update-slice_fusion.2
  632.4 1.0 slice_dynamic-update-slice_fusion.1
  633.4 1.0 slice_dynamic-update-slice_fusion
  634.4 54.7 %reduce-scatter.9.cloned.1.call-done = bf16[80,3840]{1,0:T(8,128)(2,1)} async-done(((bf16[640,3840]{1,0:T(8,128)(2,1)}), bf16[80,3840]{1,0:T(8,128)(2,1)}) %reduce-scatter.9.cloned.1.call-update) | async-done | bytes 614416 | tf_op jit(solution)/shard_map/reduce_scatter | solution.py:383
  689.1 1.0 slice_dynamic-update-slice_fusion.7
  690.0 1.0 slice_dynamic-update-slice_fusion.6
  691.0 1.0 slice_dynamic-update-slice_fusion.5
  692.0 1.1 pad_maximum_fusion.3
  693.1 1.1 pad_maximum_fusion.2
  (37 shorter events, 0.4 us)
Async XLA Ops:
  7.2 3.8 copy-start.2
  7.2 4.0 copy-start.3
  7.2 543.7 %reduce-scatter.11.cloned.1.call-start = ((), (), s32[]{:S(2)}) async-start(), calls=%async_computation.8 | async-start | bytes 3686400 | tf_op jit(solution)/shard_map/reduce_scatter | solution.py:383
  7.2 6.2 slice-start
  11.0 1.2 copy-start.4
  11.1 2.3 slice-start.1
  11.6 5.1 copy-start.6
  12.2 4.5 copy-start.5
  244.2 307.6 %reduce-scatter.7.cloned.1.call-start = ((), (), s32[]{:S(2)}) async-start(), calls=%async_computation.6 | async-start | bytes 3686400 | tf_op jit(solution)/shard_map/reduce_scatter | solution.py:383
  382.2 44.0 %copy-start = (bf16[1280,640]{1,0:T(8,128)(2,1)S(1)}, bf16[1280,640]{1,0:T(8,128)(2,1)}, u32[]{:S(2)}) copy-start(bf16[1280,640]{1,0:T(8,128)(2,1)} %get-tuple-element.66) | copy-start | bytes 4915204
  426.2 128.6 %reduce-scatter.17.cloned.1.call-start = ((), (), s32[]{:S(2)}) async-start(), calls=%async_computation.11 | async-start | bytes 4608000 | tf_op jit(solution)/shard_map/reduce_scatter | solution.py:383
  430.2 62.9 %copy-start.1 = (bf16[1280,640]{1,0:T(8,128)(2,1)S(1)}, bf16[1280,640]{1,0:T(8,128)(2,1)}, u32[]{:S(2)}) copy-start(bf16[1280,640]{1,0:T(8,128)(2,1)} %get-tuple-element.64) | copy-start | bytes 4915204
  430.3 143.5 %reduce-scatter.15.cloned.1.call-start = ((), (), s32[]{:S(2)}) async-start(), calls=%async_computation.10 | async-start | bytes 4608000 | tf_op jit(solution)/shard_map/reduce_scatter | solution.py:383
  497.1 134.4 %reduce-scatter.13.cloned.1.call-start = ((), (), s32[]{:S(2)}) async-start(), calls=%async_computation.9 | async-start | bytes 5529600 | tf_op jit(solution)/shard_map/reduce_scatter | solution.py:383
  497.7 191.4 %reduce-scatter.9.cloned.1.call-start = ((), (), s32[]{:S(2)}) async-start(), calls=%async_computation.7 | async-start | bytes 5529600 | tf_op jit(solution)/shard_map/reduce_scatter | solution.py:383
Sparse Core Ops, SparseCore 0:
  244.3 46.3 reduce-scatter.10
  426.3 46.3 reduce-scatter.6
  475.1 48.4 reduce-scatter.16
  525.7 47.9 reduce-scatter.14
  575.9 55.4 reduce-scatter.12
  633.6 55.4 reduce-scatter.8

commit v2 on v1

--- a/solution.py
+++ b/solution.py
@@ -42,29 +42,28 @@
 
 
 ZS, CORES = 4, 2
-GU_ROWS, D_ROWS = D // 8, FF // 8
+ROWS = D // 8
 
 
 def pieces_of():
     out = []
-    for buffer in range(4):
-        for n in range(10 if buffer % 2 == 0 else 5):
-            width = 640 if buffer % 2 == 0 else 128
-            out.append((buffer, pl.ds(n * width, width), n % 2))
+    for buffer in range(2):
+        for n in range(2 * BLOCKS):
+            out.append((buffer, pl.ds(n * BLOCK, BLOCK), n % 2))
     return out
 
 
 PIECES = pieces_of()
 
 
-def gate_up_kernel(sub, a_ref, gu0, d0, gu1, d1, gu_ref, p_ref, o0, o1, o2, o3, b0, b1, b2, b3, own_sem, out_sem, send_z, send_x, send_d, arrive, crossed):
+def gate_up_kernel(tile, sub, x_ref, wg, wu, gu_ref, p_ref, a_out, o0, o1, b0, b1, a_ref, own_sem, out_sem, send_z, send_x, send_d, arrive, crossed):
     r, dp = lax.axis_index("rep"), lax.axis_index("dp")
     z, k = dp // 2, dp % 2
     relay = r % 2 == k
     side = r // 2
-    buffers, outs, shards = (b0, b1, b2, b3), (o0, o1, o2, o3), (gu0, d0, gu1, d1)
+    buffers, outs = (b0, b1), (o0, o1)
     step = pl.program_id(0) * pl.num_programs(1) + pl.program_id(1)
-    steps = BLOCKS * (TOKENS // a_ref.shape[0])
+    steps = BLOCKS * (TOKENS // tile)
     count = len(PIECES)
 
     def send(q, at, to, sem, to_sem):
@@ -131,9 +130,14 @@
 
     @pl.when(step == 0)
     def _():
-        own = [pltpu.make_async_copy(shards[n], buffers[n].at[z, k], own_sem.at[n]) for n in range(4)]
-        for copy in own:
-            copy.start()
+        for n in range(2):
+            for j in range(BLOCKS):
+                for m in range(2):
+                    pltpu.make_async_copy(
+                        (wg, wu)[m].at[n, :, pl.ds(j * BLOCK, BLOCK)],
+                        buffers[n].at[z, k, :, pl.ds((2 * j + m) * BLOCK, BLOCK)],
+                        own_sem.at[n],
+                    ).start()
         barrier = pltpu.get_barrier_semaphore()
         for n in (1, 2, 3):
             pl.semaphore_signal(
@@ -142,8 +146,9 @@
             pl.semaphore_signal(barrier, inc=1, device_id=(lax.rem(r + n, 4), dp), device_id_type=pl.DeviceIdType.MESH)
         pl.semaphore_signal(barrier, inc=1, device_id=(r, z * 2 + 1 - k), device_id_type=pl.DeviceIdType.MESH)
         pl.semaphore_wait(barrier, 7)
-        for copy in own:
-            copy.wait()
+        for n in range(2):
+            ref = buffers[n].at[z, k]
+            pltpu.make_async_copy(ref, ref, own_sem.at[n]).wait()
         for q in range(count):
             along(q)
         across(0)
@@ -164,69 +169,74 @@
 
         @pl.when(step == s)
         def _():
-            across(s + 3)
-            over(s + 1)
-            arrived(s)
+            if s + 3 < count:
+                across(s + 3)
+            if s + 1 < count:
+                over(s + 1)
+            if s < count:
+                arrived(s)
 
     cols = pl.ds(pl.multiple_of(pl.program_id(0) * (2 * BLOCK), 2 * BLOCK), 2 * BLOCK)
     w = b0[:, :, :, cols].reshape(D, 2 * BLOCK)
-    for s in range(a_ref.shape[0] // sub):
+    start = pl.program_id(1) * tile
+
+    @pl.when(pl.program_id(0) == 0)
+    def _():
+        wide = x_ref[...].astype(F32)
+        a_ref[pl.ds(pl.multiple_of(start, tile), tile), :] = (wide * scale_of(wide)).astype(BF16)
+
+    @pl.when(step == TOKENS // tile)
+    def _():
+        pltpu.make_async_copy(a_ref, a_out, out_sem.at[2]).start()
+
+    for s in range(tile // sub):
         rows = pl.ds(s * sub, sub)
-        gu = nn(a_ref[rows, :], w)
+        gu = nn(a_ref[pl.ds(pl.multiple_of(start + s * sub, sub), sub), :], w)
         gu_ref[rows, :] = gu
         gate, up = gu[:, :BLOCK], gu[:, BLOCK:]
         p_ref[rows, :] = (gate * jax.nn.sigmoid(gate) * up).astype(BF16)
 
     @pl.when(step == steps - 1)
     def _():
-        for q in range(steps + 3, count):
-            across(q)
-            over(q - 2)
-        over(count - 2)
-        over(count - 1)
-        for q in range(steps, count):
-            arrived(q)
-        for n in range(4):
+        for n in range(2):
             to_hbm(n).start()
         for q in range(count):
             end(q)
-        for n in range(4):
+        for n in range(2):
             to_hbm(n).wait()
-
-
-def gate_up(a, gu0, d0, gu1, d1, tile=1024, sub=1024):
+        pltpu.make_async_copy(a_ref, a_out, out_sem.at[2]).wait()
+
+
+def gate_up(x, wg, wu, tile=1024, sub=1024):
     hbm = pl.BlockSpec(memory_space=pl.ANY)
-    wide = (ZS, CORES, GU_ROWS, 2 * FF)
-    tall = (ZS, CORES, D_ROWS, D)
+    wide = (ZS, CORES, ROWS, 2 * FF)
     count = len(PIECES)
+    last = TOKENS // tile - 1
     dma = pltpu.SemaphoreType.DMA
     return pl.pallas_call(
-        functools.partial(gate_up_kernel, sub),
+        functools.partial(gate_up_kernel, tile, sub),
         grid=(BLOCKS, TOKENS // tile),
-        in_specs=[pl.BlockSpec((tile, D), lambda j, i: (i, 0)), hbm, hbm, hbm, hbm],
+        in_specs=[pl.BlockSpec((tile, D), lambda j, i: (jnp.where(j == 0, i, last), 0)), hbm, hbm],
         out_specs=[
             pl.BlockSpec((tile, 2 * BLOCK), lambda j, i: (i, j)),
             pl.BlockSpec((tile, BLOCK), lambda j, i: (i, j)),
             hbm,
             hbm,
             hbm,
-            hbm,
         ],
         out_shape=[
             jax.ShapeDtypeStruct((TOKENS, 2 * FF), F32),
             jax.ShapeDtypeStruct((TOKENS, FF), BF16),
+            jax.ShapeDtypeStruct((TOKENS, D), BF16),
             jax.ShapeDtypeStruct(wide, BF16),
-            jax.ShapeDtypeStruct(tall, BF16),
             jax.ShapeDtypeStruct(wide, BF16),
-            jax.ShapeDtypeStruct(tall, BF16),
         ],
         scratch_shapes=[
             pltpu.VMEM(wide, BF16),
-            pltpu.VMEM(tall, BF16),
             pltpu.VMEM(wide, BF16),
-            pltpu.VMEM(tall, BF16),
-            dma((4,)),
-            dma((4,)),
+            pltpu.VMEM((TOKENS, D), BF16),
+            dma((2,)),
+            dma((3,)),
             dma((count,)),
             dma((count, 3)),
             dma((count,)),
@@ -238,18 +248,22 @@
         ),
         cost_estimate=cost(2 * MM, TOKENS * FF * 10),
         name="gate_up",
-    )(a, gu0, d0, gu1, d1)
-
-
-def down_kernel(p_ref, w_ref, h_ref, out_ref, a_ref):
-    y = nn(p_ref[...], w_ref[...]).astype(BF16)
+    )(x, wg, wu)
+
+
+def down_kernel(p_ref, w_ref, h_ref, out_ref, a_ref, across):
+    @pl.when(pl.program_id(0) == 0)
+    def _():
+        across[...] = w_ref[...].T
+
+    y = nt(across[...], p_ref[...]).T.astype(BF16)
     h = h_ref[...] + y
     out_ref[...] = h
     wide = h.astype(F32)
     a_ref[...] = (wide * scale_of(wide)).astype(BF16)
 
 
-def down(p, w, h, tile=512):
+def down(p, w, h, tile=1024):
     row = pl.BlockSpec((tile, D), lambda i: (i, 0))
     return pl.pallas_call(
         down_kernel,
@@ -261,19 +275,26 @@
         ],
         out_specs=[row, row],
         out_shape=[jax.ShapeDtypeStruct((TOKENS, D), BF16)] * 2,
+        scratch_shapes=[pltpu.VMEM((D, FF), BF16)],
         compiler_params=params("arbitrary"),
         cost_estimate=cost(MM, TOKENS * FF * 2),
         name="down",
     )(p, w, h)
 
 
-def back_kernel(sub, again, dy_ref, wd_ref, a_ref, gu_ref, dgu_ref, dw_ref, dd_ref, acc, accd, p_ref):
+def back_kernel(sub, again, with_d, joins, dy_ref, wd_ref, a_ref, gu_ref, *rest):
+    dgu_ref, *rest = rest[1:] if joins else rest
+    if with_d:
+        dw_ref, dd_ref, acc, p_ref, accd = rest
+    else:
+        dw_ref, acc = rest
     i = pl.program_id(1)
 
     @pl.when(i == 0)
     def _():
         acc[...] = jnp.zeros_like(acc)
-        accd[...] = jnp.zeros_like(accd)
+        if with_d:
+            accd[...] = jnp.zeros_like(accd)
 
     for s in range(dy_ref.shape[0] // sub):
         rows = pl.ds(s * sub, sub)
@@ -285,21 +306,26 @@
             gate, up = gu_ref[rows, :BLOCK], gu_ref[rows, BLOCK:]
         sig = jax.nn.sigmoid(gate)
         silu = gate * sig
-        p_ref[rows, :] = (silu * up).astype(BF16)
+        if with_d:
+            p_ref[rows, :] = (silu * up).astype(BF16)
         dgu_ref[rows, :BLOCK] = (dp * up * (sig * (1.0 + gate * (1.0 - sig)))).astype(BF16)
         dgu_ref[rows, BLOCK:] = (dp * silu).astype(BF16)
     acc[...] += tn(a_ref[...], dgu_ref[...])
-    accd[...] += tn(p_ref[...], dy_ref[...])
+    if with_d:
+        accd[...] += tn(p_ref[...], dy_ref[...])
 
     @pl.when(i == pl.num_programs(1) - 1)
     def _():
         dw_ref[...] = acc[...].astype(BF16)
-        dd_ref[...] = accd[...].astype(BF16)
-
-
-def back(dy, wd, a, gu, again, first, blocks, tile=1024, sub=512):
+        if with_d:
+            dd_ref[...] = accd[...].astype(BF16)
+
+
+def back(dy, wd, a, gu, again, with_d, first, blocks, joins=None, tile=1024, sub=512):
+    spare = [jax.ShapeDtypeStruct((FF, D), BF16)] if with_d else []
+    before = [] if joins is None else [joins]
     return pl.pallas_call(
-        functools.partial(back_kernel, sub, again),
+        functools.partial(back_kernel, sub, again, with_d, bool(before)),
         grid=(blocks, TOKENS // tile),
         in_specs=[
             pl.BlockSpec((tile, D), lambda j, i: (i, 0)),
@@ -308,31 +334,53 @@
             pl.BlockSpec((D, 2 * BLOCK), lambda j, i: (0, first + j))
             if again
             else pl.BlockSpec((tile, 2 * BLOCK), lambda j, i: (i, first + j)),
+            *[pl.BlockSpec(memory_space=pl.ANY) for _ in before],
         ],
         out_specs=[
             pl.BlockSpec((tile, 2 * BLOCK), lambda j, i: (i, j)),
             pl.BlockSpec((D, 2 * BLOCK), lambda j, i: (0, j)),
-            pl.BlockSpec((BLOCK, D), lambda j, i: (j, 0)),
+            *[pl.BlockSpec((BLOCK, D), lambda j, i: (first + j, 0)) for _ in spare],
         ],
         out_shape=[
             jax.ShapeDtypeStruct((TOKENS, 2 * BLOCK * blocks), BF16),
             jax.ShapeDtypeStruct((D, 2 * BLOCK * blocks), BF16),
-            jax.ShapeDtypeStruct((BLOCK * blocks, D), BF16),
+            *spare,
         ],
         scratch_shapes=[
             pltpu.VMEM((D, 2 * BLOCK), F32),
-            pltpu.VMEM((BLOCK, D), F32),
-            pltpu.VMEM((tile, BLOCK), BF16),
+            *([pltpu.VMEM((tile, BLOCK), BF16), pltpu.VMEM((BLOCK, D), F32)] if with_d else []),
         ],
         compiler_params=params("arbitrary", "arbitrary"),
         cost_estimate=cost((6 if again else 4) * MM * blocks // BLOCKS, TOKENS * FF * (4 if again else 12) * blocks // BLOCKS),
+        input_output_aliases={4: 2} if before else {},
         name="back",
-    )(dy, wd, a, gu)
+    )(dy, wd, a, gu, *before)
+
+
+def grad_down_kernel(p_ref, dy_ref, dw_ref):
+    dw_ref[:, :512] = tn(p_ref[...], dy_ref[:, :512]).astype(BF16)
+    dw_ref[:, 512:] = tn(dy_ref[:, 512:], p_ref[...]).T.astype(BF16)
+
+
+def grad_down(p, dy):
+    return pl.pallas_call(
+        grad_down_kernel,
+        grid=(BLOCKS,),
+        in_specs=[
+            pl.BlockSpec((TOKENS, BLOCK), lambda j: (0, j)),
+            pl.BlockSpec((TOKENS, D), lambda j: (0, 0), pipeline_mode=pl.Buffered(1)),
+        ],
+        out_specs=pl.BlockSpec((BLOCK, D), lambda j: (j, 0)),
+        out_shape=jax.ShapeDtypeStruct((FF, D), BF16),
+        compiler_params=params("arbitrary"),
+        cost_estimate=cost(MM, TOKENS * FF * 2),
+        name="grad_down",
+    )(p, dy)
 
 
 def grad_in_kernel(split, one_ref, two_ref, w_ref, h_ref, dy_ref, dh_ref):
-    da = nt(one_ref[...], w_ref[:, :split]) + nt(two_ref[...], w_ref[:, split:])
-    da = da.astype(BF16).astype(F32)
+    da = nt(w_ref[:, :split], one_ref[...]) + nt(w_ref[:, split:], two_ref[...])
+    da = da.T.astype(BF16).astype(F32)
     wide = h_ref[...].astype(F32)
     scale = scale_of(wide)
     dot = jnp.mean(da * wide, -1, keepdims=True)
@@ -361,19 +409,6 @@
     )(one, two, w, h, dy)
 
 
-def normed(h):
-    wide = h.astype(F32)
-    return (wide * scale_of(wide)).astype(BF16)
-
-
-def beside(gate, up):
-    parts = []
-    for j in range(BLOCKS):
-        cols = slice(j * BLOCK, (j + 1) * BLOCK)
-        parts += [gate[:, cols], up[:, cols]]
-    return jnp.concatenate(parts, 1)
-
-
 def apart(both):
     parts = [both[:, j * BLOCK : (j + 1) * BLOCK] for j in range(2 * BLOCKS)]
     return jnp.concatenate(parts[0::2], 1), jnp.concatenate(parts[1::2], 1)
@@ -383,28 +418,40 @@
     return lax.psum_scatter(dw, "dp", scatter_dimension=0, tiled=True)
 
 
-SPLIT = 2
+FIRST = 3
 
 
 def solution(mesh):
-    def backward(dy, wd, a, gu, again, w, h):
-        one, dw_one, dd_one = back(dy, wd, a, gu, again, 0, SPLIT)
-        dy, dw_one, dd_one = lax.optimization_barrier((dy, dw_one, dd_one))
-        two, dw_two, dd_two = back(dy, wd, a, gu, again, SPLIT, BLOCKS - SPLIT)
-        dy, dw_two, dd_two = lax.optimization_barrier((dy, dw_two, dd_two))
-        by_gu = jnp.concatenate([scatter(dw_one), scatter(dw_two)], 1)
-        by_d = scatter(jnp.concatenate([dd_one, dd_two], 0))
-        return grad_in(one, two, w, h, dy), apart(by_gu), by_d
+    def gathered(w):
+        return lax.all_gather(w, "dp", axis=0, tiled=True)
 
     def step(x, dy, w_gate, w_up, w_down):
         h0, dy = x[0], dy[0]
-        a0 = normed(h0)
-        gu0, p0, w0, d0, w1, d1 = gate_up(a0, beside(w_gate[0], w_up[0]), w_down[0], beside(w_gate[1], w_up[1]), w_down[1])
+        d0, d1 = gathered(w_down[0]), gathered(w_down[1])
+        gu0, p0, a0, w0, w1 = gate_up(h0, w_gate, w_up)
         w0, w1 = w0.reshape(D, 2 * FF), w1.reshape(D, 2 * FF)
-        d0, d1 = d0.reshape(FF, D), d1.reshape(FF, D)
         h1, a1 = down(p0, d0, h0)
-        dh1, (g1, u1), by_d1 = backward(dy, d1, a1, w1, True, w1, h1)
-        dx, (g0, u0), by_d0 = backward(dh1, d0, a0, gu0, False, w0, h0)
+
+        one1, dw, dd = back(dy, d1, a1, w1, True, True, 0, FIRST)
+        by_one1 = scatter(dw)
+        two1, dw, dd = back(dy, d1, a1, w1, True, True, FIRST, BLOCKS - FIRST, dd)
+        by_two1 = scatter(dw)
+        by_d1 = scatter(dd)
+        one1, by_one1 = lax.optimization_barrier((one1, by_one1))
+        dh1 = grad_in(one1, two1, w1, h1, dy)
+
+        dd = grad_down(p0, dh1)
+        by_d0 = scatter(dd)
+        dh1, dd, by_two1 = lax.optimization_barrier((dh1, dd, by_two1))
+        one0, dw = back(dh1, d0, a0, gu0, False, False, 0, FIRST)
+        by_one0 = scatter(dw)
+        dh1, dw, by_d1 = lax.optimization_barrier((dh1, dw, by_d1))
+        two0, dw = back(dh1, d0, a0, gu0, False, False, FIRST, BLOCKS - FIRST)
+        by_two0 = scatter(dw)
+        one0, dw, by_d0 = lax.optimization_barrier((one0, dw, by_d0))
+        dx = grad_in(one0, two0, w0, h0, dh1)
+        g0, u0 = apart(jnp.concatenate([by_one0, by_two0], 1))
+        g1, u1 = apart(jnp.concatenate([by_one1, by_two1], 1))
         return dx[None], jnp.stack([g0, g1]), jnp.stack([u0, u1]), jnp.stack([by_d0, by_d1])
 
     tokens = P(("rep", "dp"), None, None)

time: 710 us -> 578 us (0.81)
  waiting for transfers between devices: 130 us -> 39.2 us
  Pallas kernels: 525 us -> 504 us
  other arithmetic: 19.4 us -> 3.62 us
    reduce_scatter x6, waiting for transfers between devices: 129 us -> 37.8 us  [scatter(): return lax.psum_scatter(dw, 'dp', scatter_dimension=0, tiled=True)]
    pallas_call x2, Pallas kernels: 105 us -> 93.7 us  [grad_in(): pl.pallas_call(functools.partial(grad_in_kernel, split), grid=(TOKENS //...]
    concatenate x2 -> x0, other arithmetic: 7.94 us -> none  [backward(): by_d = scatter(jnp.concatenate([dd_one, dd_two], 0))]
    pallas_call x5 -> x6, Pallas kernels: 391 us -> 383 us  [the longest x4 234 us: back(): pl.pallas_call(functools.partial(back_kernel, sub, again, with_d, bool(be...]
  transfers between devices with their start and end apart: 6 -> 8, of which waited for: 3 -> 2; matrix products, arithmetic and copies ran while one was open for 2% -> 1% of each run, Pallas kernels for 42% -> 73%
where the time goes in v2:
time: 578 us; the launch traced here: 571 us
  Pallas kernels  504 us (87%)
  waiting for transfers between devices  39.2 us (7%)
  between operations  14.7 us (3%)
  local copies, waits for them, and re-layouts  9.15 us (2%)
    pallas_call x4, Pallas kernels, back(): pl.pallas_call(functools.partial(back_kernel, sub, again, with_d, bool(be...  234 us
    pallas_call x1, Pallas kernels, gate_up(): pl.pallas_call(functools.partial(gate_up_kernel, tile, sub), grid=(BLOCKS...  125 us
    pallas_call x2, Pallas kernels, grad_in(): pl.pallas_call(functools.partial(grad_in_kernel, split), grid=(TOKENS //...  93.7 us
    reduce_scatter x6, waiting for transfers between devices, scatter(): return lax.psum_scatter(dw, 'dp', scatter_dimension=0, tiled=True)  37.8 us
    pallas_call x1, Pallas kernels, down(): pl.pallas_call(down_kernel, grid=(TOKENS // tile,), in_specs=[pl.BlockSpe...  26.5 us
    pallas_call x1, Pallas kernels, grad_down(): pl.pallas_call(grad_down_kernel, grid=(BLOCKS,), in_specs=[pl.BlockSpec((...  23.9 us
  transfers between devices with their start and end apart: 8, of which 2 were waited for; matrix products, arithmetic and copies ran while one was open for 1% of the time, Pallas kernels for 73%

profile of v2, /device:TPU:0, one launch (start us, length us, event | category | flops | bytes accessed | tf_op | source)
XLA Modules:
  0.0 570.8 jit_solution(9809014904845549011)
XLA Ops:
  7.2 0.0 all-gather.7.cloned.1.call-start
  7.2 2.2 fusion
  9.4 0.0 all-gather.7.cloned.1.call-update
  9.5 0.0 all-gather.5.cloned.1.call-start
  9.5 0.7 all-gather.5.cloned.1.call-update
  10.2 0.0 reduce-scatter.7.cloned.1.call-start
  10.3 125.4 %gate_up.1 = (f32[4096,6400]{1,0:T(8,128)}, bf16[4096,3200]{1,0:T(8,128)(2,1)}, bf16[4096,640]{1,0:T(8,128)(2,1)}, bf16[4,2,80,6400]{3,2,1,0:T(8,128)(2,1)}, bf16[4,2,80,6400]{3,2,1,0:T(8,128)(2,1)}) custom-call(bf16[4096,640]{1,0:T(8,128)(2,1)} %bitcast.25, bf16[2,80,3200]{2,1,0:T(8,128)(2,1)} %wg.1, bf16[2,80,3200]{2,1,0:T(8,128)(2,1)} %wu.1), custom_call_target="tpu_custom_call" | custom-call | flops 33554432000 | bytes 131072000 | tf_op jit(solution)/shard_map/gate_up/pallas_call | solution.py:216
  135.7 0.0 all-gather.7.cloned.1.call-done
  135.7 26.5 %down.1 = (bf16[4096,640]{1,0:T(8,128)(2,1)}, bf16[4096,640]{1,0:T(8,128)(2,1)}) custom-call(bf16[4096,3200]{1,0:T(8,128)(2,1)} %get-tuple-element.29.p_ref, bf16[3200,640]{1,0:T(8,128)(2,1)} %bitcast.13, bf16[4096,640]{1,0:T(8,128)(2,1)} %bitcast.26), custom_call_target="tpu_custom_call" | custom-call | flops 16777216000 | bytes 26214400 | tf_op jit(solution)/shard_map/down/pallas_call | solution.py:268
  162.2 0.0 all-gather.5.cloned.1.call-done
  162.2 85.2 %back.4 = (bf16[4096,3840]{1,0:T(8,128)(2,1)}, bf16[640,3840]{1,0:T(8,128)(2,1)}, bf16[3200,640]{1,0:T(8,128)(2,1)}) custom-call(bf16[4096,640]{1,0:T(8,128)(2,1)} %bitcast.22, bf16[3200,640]{1,0:T(8,128)(2,1)} %bitcast.28, bf16[4096,640]{1,0:T(8,128)(2,1)} %get-tuple-element.30.a_ref, bf16[640,6400]{1,0:T(8,128)(2,1)} %bitcast.31), custom_call_target="tpu_custom_call" | custom-call | flops 60397977600 | bytes 31457280 | tf_op jit(solution)/shard_map/back/pallas_call | solution.py:327
  247.4 0.0 reduce-scatter.7.cloned.1.call-update
  247.4 0.0 reduce-scatter.9.cloned.1.call-start
  247.5 58.7 %back.5 = (bf16[4096,2560]{1,0:T(8,128)(2,1)}, bf16[640,2560]{1,0:T(8,128)(2,1)}, bf16[3200,640]{1,0:T(8,128)(2,1)}) custom-call(bf16[4096,640]{1,0:T(8,128)(2,1)} %bitcast.23, bf16[3200,640]{1,0:T(8,128)(2,1)} %bitcast.29, bf16[4096,640]{1,0:T(8,128)(2,1)} %get-tuple-element.30.a_ref, bf16[640,6400]{1,0:T(8,128)(2,1)} %bitcast.32, ...), custom_call_target="tpu_custom_call", output_to_operand_aliasing={{2}: (4, {})} | custom-call | flops 40265318400 | bytes 20971520 | tf_op jit(solution)/shard_map/back/pallas_call | solution.py:327
  306.2 0.0 reduce-scatter.9.cloned.1.call-update
  306.2 0.0 reduce-scatter.11.cloned.1.call-start
  306.3 0.5 reduce-scatter.11.cloned.1.call-update
  306.8 0.0 reduce-scatter.13.cloned.1.call-start
  306.9 8.3 %reduce-scatter.7.cloned.1.call-done = bf16[80,3840]{1,0:T(8,128)(2,1)} async-done(((bf16[640,3840]{1,0:T(8,128)(2,1)}), bf16[80,3840]{1,0:T(8,128)(2,1)}) %reduce-scatter.7.cloned.1.call-update) | async-done | bytes 614416 | tf_op jit(solution)/shard_map/reduce_scatter | solution.py:418
  315.2 46.9 %grad_in.2.dy_ref = bf16[4096,640]{1,0:T(8,128)(2,1)} custom-call(bf16[4096,3840]{1,0:T(8,128)(2,1)} %get-tuple-element.34.one_ref, bf16[4096,2560]{1,0:T(8,128)(2,1)} %get-tuple-element.36.two_ref, bf16[640,6400]{1,0:T(8,128)(2,1)} %bitcast.33, bf16[4096,640]{1,0:T(8,128)(2,1)} %get-tuple-element.37.h_ref, bf16[4096,640]{1,0:T(8,128)(2,1)} %bitcast.24), custom_call_target="tpu_custom_call" | custom-call | flops 33554432000 | bytes 52428800 | tf_op jit(solution)/shard_map/grad_in/pallas_call | solution.py:394
  362.0 23.9 %grad_down.1 = bf16[3200,640]{1,0:T(8,128)(2,1)} custom-call(bf16[4096,3200]{1,0:T(8,128)(2,1)} %get-tuple-element.29.p_ref, bf16[4096,640]{1,0:T(8,128)(2,1)} %grad_in.2.dy_ref), custom_call_target="tpu_custom_call" | custom-call | flops 16777216000 | bytes 26214400 | tf_op jit(solution)/shard_map/grad_down/pallas_call | solution.py:366
  386.0 0.0 reduce-scatter.13.cloned.1.call-update
  386.0 0.3 reduce-scatter.15.cloned.1.call-start
  386.3 0.0 reduce-scatter.9.cloned.1.call-done
  386.3 53.0 %back.6 = (bf16[4096,3840]{1,0:T(8,128)(2,1)}, bf16[640,3840]{1,0:T(8,128)(2,1)}) custom-call(bf16[4096,640]{1,0:T(8,128)(2,1)} %grad_in.2.dy_ref, bf16[3200,640]{1,0:T(8,128)(2,1)} %bitcast.14, bf16[4096,640]{1,0:T(8,128)(2,1)} %get-tuple-element.40.a_ref, f32[4096,6400]{1,0:T(8,128)} %get-tuple-element.41.gu_ref), custom_call_target="tpu_custom_call" | custom-call | flops 40265318400 | bytes 94371840 | tf_op jit(solution)/shard_map/back/pallas_call | solution.py:327
  439.3 0.0 reduce-scatter.15.cloned.1.call-update
  439.4 0.0 copy-start
  439.4 0.0 reduce-scatter.17.cloned.1.call-start
  439.4 0.0 reduce-scatter.11.cloned.1.call-done
  439.4 37.1 %back.7 = (bf16[4096,2560]{1,0:T(8,128)(2,1)}, bf16[640,2560]{1,0:T(8,128)(2,1)}) custom-call(bf16[4096,640]{1,0:T(8,128)(2,1)} %grad_in.2.dy_ref, bf16[3200,640]{1,0:T(8,128)(2,1)} %bitcast.15, bf16[4096,640]{1,0:T(8,128)(2,1)} %get-tuple-element.40.a_ref, f32[4096,6400]{1,0:T(8,128)} %get-tuple-element.41.gu_ref), custom_call_target="tpu_custom_call" | custom-call | flops 26843545600 | bytes 62914560 | tf_op jit(solution)/shard_map/back/pallas_call | solution.py:327
  476.5 0.0 copy-start.1
  476.5 0.0 reduce-scatter.17.cloned.1.call-update
  476.5 0.0 copy-done
  476.6 1.0 slice_dynamic-update-slice_fusion.11
  477.7 1.0 slice_dynamic-update-slice_fusion.10
  478.6 0.0 reduce-scatter.13.cloned.1.call-done
  478.7 0.0 copy-done.1
  478.7 2.1 pad_maximum_fusion.2
  480.8 46.9 %grad_in.3 = bf16[4096,640]{1,0:T(8,128)(2,1)} custom-call(bf16[4096,3840]{1,0:T(8,128)(2,1)} %get-tuple-element.47.one_ref, bf16[4096,2560]{1,0:T(8,128)(2,1)} %get-tuple-element.48.two_ref, bf16[640,6400]{1,0:T(8,128)(2,1)} %bitcast.30, bf16[4096,640]{1,0:T(8,128)(2,1)} %bitcast.27, bf16[4096,640]{1,0:T(8,128)(2,1)} %grad_in.2.dy_ref), custom_call_target="tpu_custom_call" | custom-call | flops 33554432000 | bytes 52428800 | tf_op jit(solution)/shard_map/grad_in/pallas_call | solution.py:394
  527.6 0.0 reduce-scatter.15.cloned.1.call-done
  527.6 1.0 slice_dynamic-update-slice_fusion.4
  528.6 1.0 slice_dynamic-update-slice_fusion.3
  529.6 1.0 slice_dynamic-update-slice_fusion.2
  530.6 29.5 %reduce-scatter.17.cloned.1.call-done = bf16[80,2560]{1,0:T(8,128)(2,1)} async-done(((bf16[640,2560]{1,0:T(8,128)(2,1)}), bf16[80,2560]{1,0:T(8,128)(2,1)}) %reduce-scatter.17.cloned.1.call-update) | async-done | bytes 409616 | tf_op jit(solution)/shard_map/reduce_scatter | solution.py:418
  560.0 1.0 slice_dynamic-update-slice_fusion.1
  561.0 1.0 slice_dynamic-update-slice_fusion
  562.0 1.5 pad_maximum_fusion
  (3 shorter events, 0.1 us)
Async XLA Ops:
  7.2 128.5 %all-gather.7.cloned.1.call-start = ((), (), s32[]{:S(2)}) async-start(), calls=%async_computation.13 | async-start | bytes 4608000 | tf_op jit(solution)/shard_map/all_gather | solution.py:426
  9.5 152.7 %all-gather.5.cloned.1.call-start = ((), (), s32[]{:S(2)}) async-start(), calls=%async_computation.12 | async-start | bytes 4608000 | tf_op jit(solution)/shard_map/all_gather | solution.py:426
  10.2 304.9 %reduce-scatter.7.cloned.1.call-start = ((), (), s32[]{:S(2)}) async-start(), calls=%async_computation.6 | async-start | bytes 5529600 | tf_op jit(solution)/shard_map/reduce_scatter | solution.py:418
  247.4 138.9 %reduce-scatter.9.cloned.1.call-start = ((), (), s32[]{:S(2)}) async-start(), calls=%async_computation.7 | async-start | bytes 3686400 | tf_op jit(solution)/shard_map/reduce_scatter | solution.py:418
  306.2 133.2 %reduce-scatter.11.cloned.1.call-start = ((), (), s32[]{:S(2)}) async-start(), calls=%async_computation.8 | async-start | bytes 4608000 | tf_op jit(solution)/shard_map/reduce_scatter | solution.py:418
  306.8 171.8 %reduce-scatter.13.cloned.1.call-start = ((), (), s32[]{:S(2)}) async-start(), calls=%async_computation.9 | async-start | bytes 4608000 | tf_op jit(solution)/shard_map/reduce_scatter | solution.py:418
  386.0 141.6 %reduce-scatter.15.cloned.1.call-start = ((), (), s32[]{:S(2)}) async-start(), calls=%async_computation.10 | async-start | bytes 5529600 | tf_op jit(solution)/shard_map/reduce_scatter | solution.py:418
  439.4 37.2 %copy-start = (bf16[80,3840]{1,0:T(8,128)(2,1)S(1)}, bf16[80,3840]{1,0:T(8,128)(2,1)}, u32[]{:S(2)}) copy-start(bf16[80,3840]{1,0:T(8,128)(2,1)} %reduce-scatter.7.cloned.1.call-done) | copy-start | bytes 1843204
  439.4 120.7 %reduce-scatter.17.cloned.1.call-start = ((), (), s32[]{:S(2)}) async-start(), calls=%async_computation.11 | async-start | bytes 3686400 | tf_op jit(solution)/shard_map/reduce_scatter | solution.py:418
  476.5 2.2 copy-start.1
Sparse Core Ops, SparseCore 0:
  10.2 73.9 all-gather.6
  86.4 48.7 all-gather.4
  247.6 67.5 reduce-scatter.6
  317.3 41.0 reduce-scatter.8
  360.6 48.4 reduce-scatter.10
  411.9 47.9 reduce-scatter.12
  462.2 55.4 reduce-scatter.14
  520.0 39.9 reduce-scatter.16
